TPU v7x, 128 devices: a whole 4x4x4 slice. The times are simulated.
128 devices in a mesh: gx: 4 (over z_lo, core), gy: 16 (over x, y), gz: 2 (over z_hi).
Axes of the slice: x: 4, y: 4, z: 4 (z_hi: 2, z_lo: 2; z = z_hi * 2 + z_lo), core: 2. Of those that a mesh axis runs over, the one named last changes fastest.
Arguments:
- eigvecs: bfloat16 [64, 128, 96, 512], P('gx', 'gy', 'gz'), may hold values from -7 to 7, as said below
- material: float32 [2, 64, 128, 96], P(None, 'gx', 'gy', 'gz'), may hold values from 0.5 to 2
Outputs:
- stiffness: float32 [512, 512], P(('gx', 'gy', 'gz'))
- mass_matrix: float32 [512, 512], P(('gx', 'gy', 'gz'))
Inputs may be any that keep to these rules, and one draw needn't show every extreme that they name: `eigvecs`: entries are a rough part plus a part that varies slowly over the grid.
All inputs are finite; a program needn't handle non-finite values.
Results may differ from a plain program's by a relative error of at most 0.0003.
Values may be sent and summed in bfloat16 or wider, within the bound.
A program may use at most 128 MiB of HBM per device.

v0:
```python
import functools
import numpy as np
import jax
import jax.numpy as jnp
from jax import lax
from jax.experimental import pallas as pl
from jax.experimental.pallas import tpu as pltpu
from jax.sharding import PartitionSpec as P


def upper(cells, axis, dim):
    count = lax.axis_size(axis)
    head = lax.slice_in_dim(cells, 0, 1, axis=dim)
    return lax.ppermute(head, axis, [(i + 1, i) for i in range(count - 1)])


def taps(count, middle):
    t = middle * np.eye(count) + np.eye(count, k=1) + np.eye(count, k=-1)
    t[-1, -1] = 0.0
    return t


def rows_of(size_y, size_z):
    order = np.zeros((size_y + 1, size_z + 1), np.int64)
    base = (size_y + 1) * size_z
    for y in range(size_y + 1):
        order[y, :size_z] = y * size_z + np.arange(size_z)
        order[y, size_z] = base + y
    order[size_y, size_z] = base + -(-size_y // 16) * 16
    return order


def plane_matrix(size_y, size_z, rows):
    order = rows_of(size_y, size_z).reshape(-1)
    blocks = []
    for middle in (2.0, 4.0):
        full = np.kron(taps(size_y + 1, middle), taps(size_z + 1, middle))
        block = np.zeros((rows, rows))
        block[np.ix_(order, order)] = full
        blocks.append(block)
    return np.concatenate(blocks, 0)


def coefficients(ext, rows, cells_shape):
    size_x, size_y, size_z = cells_shape
    kappa, rho = ext[0], ext[1]
    field = kappa
    for dim in range(3):
        n = field.shape[dim]
        pad = [(1, 1) if d == dim else (0, 0) for d in range(3)]
        wide = jnp.pad(field, pad)
        lower = lax.slice_in_dim(wide, 0, n, axis=dim)
        above = lax.slice_in_dim(wide, 2, n + 2, axis=dim)
        shape = [1, 1, 1]
        shape[dim] = n
        diag = jnp.asarray(np.r_[np.full(n - 1, 2.0), 0.0].reshape(shape), jnp.float32)
        field = lower + above + diag * field
    owned = np.zeros(kappa.shape, np.float32)
    owned[:size_x, :size_y, :size_z] = 2.0
    diag = owned * kappa + field * (1.0 / 32.0)
    parts = jnp.stack([diag, kappa * (1.0 / 16.0), rho * (1.0 / 216.0)], axis=1)
    main = parts[..., :size_z].reshape(size_x + 1, 3, (size_y + 1) * size_z)
    edge = parts[:, :, :size_y, size_z]
    edge = jnp.pad(edge, ((0, 0), (0, 0), (0, -size_y % 16)))
    both = jnp.concatenate([main, edge, parts[:, :, size_y:, size_z]], axis=2)
    return jnp.pad(both, ((0, 0), (0, 5), (0, rows - both.shape[2])))


OFFSETS = [(0, 1, 0), (0, 0, 1), (1, 0, 0), (0, 1, 1), (1, 0, 1), (1, 1, 0), (1, 1, 1)]
AXES = ("gx", "gy", "gz")


def inside(offset, sign):
    ok = None
    for axis, d in zip(AXES, offset):
        if d:
            at = lax.axis_index(axis)
            here = at > 0 if sign < 0 else at < lax.axis_size(axis) - 1
            ok = here if ok is None else jnp.logical_and(ok, here)
    return ok


def device_at(offset, sign):
    return {axis: lax.axis_index(axis) + sign * d for axis, d in zip(AXES, offset) if d}


def greet_around():
    barrier = pltpu.get_barrier_semaphore()
    total = jnp.int32(0)
    for offset in OFFSETS:
        for sign in (-1, 1):
            there = inside(offset, sign)

            @pl.when(there)
            def _(offset=offset, sign=sign):
                pl.semaphore_signal(barrier, inc=1, device_id=device_at(offset, sign),
                                    device_id_type=pl.DeviceIdType.MESH)

            total = total + jnp.where(there, 1, 0)
    pl.semaphore_wait(barrier, total)


def kernel(scale, v_ref, z_ref, k_ref, t_ref, c_ref, out_ref, e_ref, corners, p0, p1, p2, p3, acc,
           own_sem, send, recv, y_send, y_recv):
    slots = (p0, p1, p2, p3)
    rows, columns = e_ref.shape[1:]
    nx, owned, _ = v_ref.shape
    planes = nx + 1
    edge = z_ref.shape[1]
    width = rows - owned - edge - 16
    y_at, z_at, c_at = owned, owned + width, owned + width + edge
    own = pltpu.make_async_copy(v_ref, e_ref.at[:nx, :owned], own_sem)
    own.start()
    places = {
        (0, 1, 0): (v_ref.at[:, :width], e_ref.at[:nx, y_at:z_at]),
        (0, 0, 1): (z_ref, e_ref.at[:nx, z_at:c_at]),
        (0, 1, 1): (k_ref, corners.at[0]),
        (1, 0, 0): (v_ref.at[0], e_ref.at[nx, :owned]),
        (1, 0, 1): (z_ref.at[0], e_ref.at[nx, z_at:c_at]),
        (1, 1, 0): (v_ref.at[0, :width], e_ref.at[nx, y_at:z_at]),
        (1, 1, 1): (k_ref, corners.at[1]),
    }
    greet_around()
    copies = {}
    y_here, y_below = (0, 1, 0), device_at((0, 1, 0), -1)

    def chunk(i):
        four = pl.ds(4 * i, 4)
        return pltpu.make_async_remote_copy(
            src_ref=v_ref.at[four, :width], dst_ref=e_ref.at[four, y_at:z_at],
            send_sem=y_send.at[i], recv_sem=y_recv.at[i],
            device_id=y_below, device_id_type=pl.DeviceIdType.MESH)

    for n, offset in ((1, (0, 0, 1)), (3, (0, 1, 1)), (0, y_here), (2, (1, 0, 0)),
                      (4, (1, 0, 1)), (5, (1, 1, 0)), (6, (1, 1, 1))):
        if offset == y_here:
            for i in range(nx // 4):
                pl.when(inside(offset, -1))(chunk(i).start)
            continue
        src, dst = places[offset]
        copies[offset] = pltpu.make_async_remote_copy(
            src_ref=src, dst_ref=dst, send_sem=send.at[n], recv_sem=recv.at[n],
            device_id=device_at(offset, -1), device_id_type=pl.DeviceIdType.MESH)
        pl.when(inside(offset, -1))(copies[offset].start)
    for offset in OFFSETS:
        src, dst = places[offset]

        @pl.when(jnp.logical_not(inside(offset, 1)))
        def _(dst=dst):
            dst[...] = jnp.zeros(dst.shape, dst.dtype)

    own.wait()
    for offset in ((0, 0, 1), (0, 1, 1)):
        pl.when(inside(offset, 1))(copies[offset].wait_recv)
    pl.when(inside(y_here, 1))(chunk(0).wait_recv)

    def fill_corner(x, row):
        e_ref[x, c_at:] = jnp.broadcast_to(row.astype(jnp.float32), (16, columns)).astype(e_ref.dtype)

    for x in range(nx):
        fill_corner(x, corners[0, x:x + 1])

    def taps_of(x, slot):
        slots[slot % 4][...] = jnp.dot(t_ref[...], e_ref[x], preferred_element_type=jnp.float32)

    def step(x, slot, two, four, ahead):
        if ahead:
            taps_of(x + 2, slot + 2)
        before, now, after = (slots[(slot + k) % 4] for k in (3, 0, 1))
        coef = c_ref[x].T
        v = e_ref[x]
        stiff = before[:rows] + after[:rows] + two * now[:rows]
        yk = coef[:, 0:1] * v.astype(jnp.float32) - coef[:, 1:2] * stiff
        mass = before[rows:] + after[rows:] + four * now[rows:]
        ym = coef[:, 2:3] * mass
        dims = (((0,), (0,)), ((), ()))
        acc[:, :columns] += lax.dot_general(v, yk.astype(jnp.bfloat16), dims, preferred_element_type=jnp.float32)
        acc[:, columns:] += lax.dot_general(v, ym.astype(jnp.bfloat16), dims, preferred_element_type=jnp.float32)

    acc[...] = jnp.zeros_like(acc)
    e_ref[planes] = jnp.zeros((rows, columns), e_ref.dtype)
    p3[...] = jnp.zeros_like(p3)
    taps_of(0, 0)
    taps_of(1, 1)
    whole = (planes - 1) // 4

    def four_steps(i, carry):
        @pl.when(i < whole - 1)
        def _():
            pl.when(inside(y_here, 1))(chunk(i + 1).wait_recv)

        @pl.when(i == whole - 1)
        def _():
            for offset in OFFSETS:
                if offset[0]:
                    pl.when(inside(offset, 1))(copies[offset].wait_recv)
            fill_corner(nx, corners[1, 0:1])

        for j in range(4):
            step(4 * i + j, j, 2.0, 4.0, True)
        return carry

    lax.fori_loop(0, whole, four_steps, 0)
    for x in range(4 * whole, planes):
        last = x == planes - 1
        step(x, x, 0.0 if last else 2.0, 0.0 if last else 4.0, x + 2 <= planes)
    for half in range(2):
        m = acc[:, half * columns:(half + 1) * columns]
        out_ref[:, half * columns:(half + 1) * columns] = (m + m.T) * scale
    for i in range(nx // 4):
        pl.when(inside(y_here, -1))(chunk(i).wait_send)
    for offset in OFFSETS:
        if offset != y_here:
            pl.when(inside(offset, -1))(copies[offset].wait_send)


def spread(axis, piece, landing, send, recv):
    count = lax.axis_size(axis)
    me = lax.axis_index(axis)
    copies = []
    for k in range(1, count):
        peer = lax.rem(me + k, count)
        copy = pltpu.make_async_remote_copy(
            src_ref=piece(peer), dst_ref=landing.at[k - 1],
            send_sem=send.at[k - 1], recv_sem=recv.at[k - 1],
            device_id={axis: peer}, device_id_type=pl.DeviceIdType.MESH)
        copy.start()
        copies.append(copy)
    return copies


def greet(axes):
    barrier = pltpu.get_barrier_semaphore()
    total = 0
    for axis in axes:
        count = lax.axis_size(axis)
        me = lax.axis_index(axis)
        for k in range(1, count):
            pl.semaphore_signal(barrier, inc=1, device_id={axis: lax.rem(me + k, count)},
                                device_id_type=pl.DeviceIdType.MESH)
        total += count - 1
    pl.semaphore_wait(barrier, total)


def reduce_kernel(cut, part, stiff_out, mass_out, rz, sa, sb, ra1, rb1, ta, tb, ra2, rb2, out,
                  *sems):
    z_send, z_recv, a1s, a1r, b1s, b1r, a2s, a2r, b2s, b2r = sems
    gx, gy, gz = (lax.axis_index(a) for a in ("gx", "gy", "gz"))
    greet(("gx", "gy", "gz"))
    first = spread("gz", lambda p: part.at[:, :, p], rz, z_send, z_recv)
    for copy in first:
        copy.wait_recv()
    held = part[:, :, gz]
    for k in range(len(first)):
        held = held + rz[k]
    sa[...] = held[..., :cut]
    sb[...] = held[..., cut:]
    a1 = spread("gy", lambda p: sa.at[:, p], ra1, a1s, a1r)
    b1 = spread("gx", lambda p: sb.at[p], rb1, b1s, b1r)
    for copy in a1:
        copy.wait_recv()
    held = sa[:, gy]
    for k in range(len(a1)):
        held = held + ra1[k]
    ta[...] = held
    a2 = spread("gx", lambda p: ta.at[p], ra2, a2s, a2r)
    for copy in b1:
        copy.wait_recv()
    held = sb[gx]
    for k in range(len(b1)):
        held = held + rb1[k]
    tb[...] = held
    b2 = spread("gy", lambda p: tb.at[p], rb2, b2s, b2r)
    for copy in a2:
        copy.wait_recv()
    held = ta[gx]
    for k in range(len(a2)):
        held = held + ra2[k]
    out[:, :cut] = held
    for copy in b2:
        copy.wait_recv()
    held = tb[gy]
    for k in range(len(b2)):
        held = held + rb2[k]
    out[:, cut:] = held
    columns = stiff_out.shape[1]
    stiff_out[...] = out[:, :columns]
    mass_out[...] = out[:, columns:]
    for copy in first + a1 + b1 + a2 + b2:
        copy.wait_send()


def reduced(part):
    nx, ny, nz = (lax.axis_size(a) for a in ("gx", "gy", "gz"))
    wide = part.shape[1]
    rows = part.shape[0] // (nx * ny * nz)
    cut = (wide * 5 // 8) // 128 * 128
    rest = wide - cut
    f32 = jnp.float32
    dma = pltpu.SemaphoreType.DMA
    vmem = pl.BlockSpec(memory_space=pltpu.VMEM)
    return pl.pallas_call(
        functools.partial(reduce_kernel, cut),
        out_shape=[jax.ShapeDtypeStruct((rows, wide // 2), f32)] * 2,
        in_specs=[vmem],
        out_specs=[vmem, vmem],
        scratch_shapes=[
            pltpu.VMEM((nz - 1, nx, ny, rows, wide), f32),
            pltpu.VMEM((nx, ny, rows, cut), f32),
            pltpu.VMEM((nx, ny, rows, rest), f32),
            pltpu.VMEM((ny - 1, nx, rows, cut), f32),
            pltpu.VMEM((nx - 1, ny, rows, rest), f32),
            pltpu.VMEM((nx, rows, cut), f32),
            pltpu.VMEM((ny, rows, rest), f32),
            pltpu.VMEM((nx - 1, rows, cut), f32),
            pltpu.VMEM((ny - 1, rows, rest), f32),
            pltpu.VMEM((rows, wide), f32),
        ] + [dma((n - 1,)) for n in (nz, nz, ny, ny, nx, nx, nx, nx, ny, ny)],
        compiler_params=pltpu.CompilerParams(collective_id=1, has_side_effects=True),
    )(part.reshape(nx, ny, nz, rows, wide))


def per_device(eigvecs, material):
    size_x, size_y, size_z, columns = eigvecs.shape
    axes = ("gx", "gy", "gz")
    devices_all = 1
    for axis in axes:
        devices_all *= lax.axis_size(axis)
    total_cells = size_x * size_y * size_z * devices_all
    ext = material
    for axis, dim in (("gz", 3), ("gy", 2), ("gx", 1)):
        ext = jnp.concatenate([ext, upper(ext, axis, dim)], axis=dim)
    edge = -(-size_y // 16) * 16
    rows = (size_y + 1) * size_z + edge + 16
    coef = coefficients(ext, rows, (size_x, size_y, size_z))
    z_layer = jnp.pad(eigvecs[:, :, 0], ((0, 0), (0, edge - size_y), (0, 0)))
    corner = eigvecs[:, 0, 0]
    matrix = jnp.asarray(plane_matrix(size_y, size_z, rows), jnp.bfloat16)
    vmem = pl.BlockSpec(memory_space=pltpu.VMEM)
    anywhere = pl.BlockSpec(memory_space=pl.ANY)
    part = pl.pallas_call(
        functools.partial(kernel, 0.5 / total_cells),
        out_shape=jax.ShapeDtypeStruct((columns, 2 * columns), jnp.float32),
        in_specs=[anywhere, vmem, vmem, vmem, vmem],
        out_specs=vmem,
        scratch_shapes=[
            pltpu.VMEM((size_x + 2, rows, columns), eigvecs.dtype),
            pltpu.VMEM((2, size_x, columns), eigvecs.dtype),
        ] + [pltpu.VMEM((2 * rows, columns), jnp.float32)] * 4 + [
            pltpu.VMEM((columns, 2 * columns), jnp.float32),
            pltpu.SemaphoreType.DMA,
            pltpu.SemaphoreType.DMA((7,)),
            pltpu.SemaphoreType.DMA((7,)),
            pltpu.SemaphoreType.DMA((size_x // 4,)),
            pltpu.SemaphoreType.DMA((size_x // 4,)),
        ],
        compiler_params=pltpu.CompilerParams(
            vmem_limit_bytes=60 * 1024 * 1024, collective_id=0, has_side_effects=True),
    )(eigvecs.reshape(size_x, size_y * size_z, columns), z_layer, corner, matrix, coef)
    return tuple(reduced(part))


def solution(mesh):
    return jax.shard_map(
        per_device,
        mesh=mesh,
        in_specs=(P("gx", "gy", "gz", None), P(None, "gx", "gy", "gz")),
        out_specs=(P(("gx", "gy", "gz"), None), P(("gx", "gy", "gz"), None)),
        check_vma=False,
    )
```

profile of v0, /device:TPU:1, one launch (start us, length us, event | category | flops | bytes accessed | tf_op | source)
XLA Modules:
  0.0 127.7 jit_solution(1010947530789154679)
XLA Ops:
  0.6 0.9 copy.68
  1.6 1.4 %collective-permute-start = (f32[2,16,8,1]{3,1,2,0:T(8,128)S(1)}, f32[2,16,8,1]{3,1,2,0:T(8,128)S(1)}, u32[]{:S(2)}, u32[]{:S(2)}) collective-permute-start(f32[2,16,8,1]{3,1,2,0:T(8,128)S(1)} %bitcast.22), channel_id=1, source_target_pairs={{1,0},{3,2},{5,4},{7,6},{9,8},{11,10},{13,12},{15,14},{17,16},{19,... | collective-permute-start | bytes 3080 | tf_op jit(solution)/shard_map/ppermute | solution.py:14
  3.1 7.4 %collective-permute-done = f32[2,16,8,1]{3,1,2,0:T(8,128)S(1)} collective-permute-done((f32[2,16,8,1]{3,1,2,0:T(8,128)S(1)}, f32[2,16,8,1]{3,1,2,0:T(8,128)S(1)}, u32[]{:S(2)}, u32[]{:S(2)}) %collective-permute-start) | collective-permute-done | bytes 1056 | tf_op jit(solution)/shard_map/ppermute | solution.py:14
  10.6 1.3 %collective-permute-start.1 = (f32[2,16,1,49]{3,1,2,0:T(8,128)S(1)}, f32[2,16,1,49]{3,1,2,0:T(8,128)S(1)}, u32[]{:S(2)}, u32[]{:S(2)}) collective-permute-start(f32[2,16,1,49]{3,1,2,0:T(8,128)S(1)} %pad_maximum_fusion.3), channel_id=1, source_target_pairs={{2,0},{4,2},{6,4},{8,6},{10,8},{12,10},{14,12},{16,14},{18,16},{20... | collective-permute-start | bytes 18824 | tf_op jit(solution)/shard_map/ppermute | solution.py:14
  11.8 3.2 %collective-permute-done.1 = f32[2,16,1,49]{3,1,2,0:T(8,128)S(1)} collective-permute-done((f32[2,16,1,49]{3,1,2,0:T(8,128)S(1)}, f32[2,16,1,49]{3,1,2,0:T(8,128)S(1)}, u32[]{:S(2)}, u32[]{:S(2)}) %collective-permute-start.1) | collective-permute-done | bytes 6304 | tf_op jit(solution)/shard_map/ppermute | solution.py:14
  15.1 4.5 %collective-permute-start.2 = (f32[2,1,9,49]{3,1,2,0:T(1,128)S(1)}, f32[2,1,9,49]{3,1,2,0:T(1,128)S(1)}, u32[]{:S(2)}, u32[]{:S(2)}) collective-permute-start(f32[2,1,9,49]{3,1,2,0:T(1,128)S(1)} %pad_maximum_fusion.4), channel_id=1, source_target_pairs={{32,0},{64,32},{96,64},{33,1},{65,33},{97,65},{34,2},{66,34},{98,6... | collective-permute-start | bytes 10592 | tf_op jit(solution)/shard_map/ppermute | solution.py:14
  19.6 0.9 slice.49
  20.5 1.4 %slice.48 = bf16[16,8,1,512]{3,2,1,0:T(2,128)(2,1)S(1)} slice(bf16[16,8,48,512]{3,2,1,0:T(8,128)(2,1)} %param.7), slice={[0:16], [0:8], [0:1], [0:512]} | slice | bytes 262144 | tf_op jit(solution)/shard_map/slice | solution.py:336
  21.9 0.6 copy.89
  22.6 0.7 pad.24.z_ref
  23.7 0.1 add_bitcast_fusion
  23.8 0.6 copy.71
  24.4 0.6 copy.72
  25.0 0.6 copy.73
  25.8 1.5 %pad_maximum_fusion = f32[17,3,9,49]{2,1,0,3:T(4,128)S(1)} fusion(f32[17,1,9,49]{2,1,0,3:T(1,128)S(1)} %copy.73, f32[17,1,9,49]{2,1,0,3:T(1,128)S(1)} %copy.72, f32[17,1,9,49]{2,1,0,3:T(1,128)S(1)} %copy.71), kind=kLoop, calls=%fused_computation | loop fusion | flops 44982 | bytes 179928 | tf_op jit(solution)/shard_map/stack | solution.py:61
  27.5 1.5 %slice.67 = f32[17,3,9,48]{2,1,0,3:T(4,128)} slice(f32[17,3,9,49]{2,1,0,3:T(4,128)S(1)} %pad_maximum_fusion), slice={[0:17], [0:3], [0:9], [0:48]} | slice | bytes 176256 | tf_op jit(solution)/shard_map/slice | solution.py:62
  29.0 2.0 %copy.82 = f32[17,3,9,48]{3,2,1,0:T(8,128)S(1)} copy(f32[17,3,9,48]{2,1,0,3:T(4,128)} %slice.67) | data formatting | bytes 176256 | tf_op jit(solution)/shard_map/reshape | solution.py:62
  31.0 0.2 reshape.40
  31.3 0.7 pad.29.c_ref
  32.1 39.4 %shard_map.86 = f32[512,1024]{1,0:T(8,128)} custom-call(bf16[16,384,512]{2,1,0:T(8,128)(2,1)} %bitcast.21, bf16[16,16,512]{2,1,0:T(8,128)(2,1)} %pad.24.z_ref, bf16[16,512]{1,0:T(8,128)(2,1)} %bitcast.24, bf16[928,464]{1,0:T(8,128)(2,1)} %constant.25.clone.t_ref, f32[17,8,464]{2,1,0:T(8,128)} %pad.29.c_ref), custom_call_target="tpu_custom_call" | custom-call | tf_op jit(solution)/shard_map/pallas_call | solution.py:341
  71.4 2.8 %reshape.39.part = f32[4,16,2,4,1024]{4,3,2,1,0:T(4,128)} reshape(f32[512,1024]{1,0:T(8,128)} %shard_map.86) | data formatting | bytes 4194304 | tf_op jit(solution)/shard_map/reshape | solution.py:320
  74.3 50.8 %shard_map.87 = (f32[4,512]{1,0:T(4,128)}, f32[4,512]{1,0:T(4,128)}) custom-call(f32[4,16,2,4,1024]{4,3,2,1,0:T(4,128)} %reshape.39.part), custom_call_target="tpu_custom_call" | custom-call | tf_op jit(solution)/shard_map/pallas_call | solution.py:302
  125.1 1.3 %copy.92 = f32[4,512]{1,0:T(4,128)} copy(f32[4,512]{1,0:T(4,128)} %get-tuple-element.7) | data formatting | bytes 16384
  126.4 1.3 %copy.93 = f32[4,512]{1,0:T(4,128)} copy(f32[4,512]{1,0:T(4,128)} %get-tuple-element.8) | data formatting | bytes 16384
  (21 shorter events, 1.0 us)
Async XLA Ops:
  0.6 22.8 %copy-start.2 = (f32[17]{0:T(128)S(1)}, f32[17]{0:T(128)}, u32[]{:S(2)}) copy-start(f32[17]{0:T(128)} %constant.40) | copy-start | bytes 208
  1.6 22.0 %copy-start.1 = (f32[9]{0:T(128)S(1)}, f32[9]{0:T(128)}, u32[]{:S(2)}) copy-start(f32[9]{0:T(128)} %constant.41) | copy-start | bytes 112
  1.6 22.0 %copy-start = (f32[17,9,49]{2,0,1:T(8,128)S(1)}, f32[17,9,49]{2,0,1:T(8,128)}, u32[]{:S(2)}) copy-start(f32[17,9,49]{2,0,1:T(8,128)} %constant.24.clone) | copy-start | bytes 89968
  1.6 22.0 %copy-start.3 = (f32[49]{0:T(128)S(1)}, f32[49]{0:T(128)}, u32[]{:S(2)}) copy-start(f32[49]{0:T(128)} %constant.42) | copy-start | bytes 592
  1.6 8.9 %collective-permute-start = (f32[2,16,8,1]{3,1,2,0:T(8,128)S(1)}, f32[2,16,8,1]{3,1,2,0:T(8,128)S(1)}, u32[]{:S(2)}, u32[]{:S(2)}) collective-permute-start(f32[2,16,8,1]{3,1,2,0:T(8,128)S(1)} %bitcast.22), channel_id=1, source_target_pairs={{1,0},{3,2},{5,4},{7,6},{9,8},{11,10},{13,12},{15,14},{17,16},{19,... | collective-permute-start | bytes 3080 | tf_op jit(solution)/shard_map/ppermute | solution.py:14
  10.6 4.5 %collective-permute-start.1 = (f32[2,16,1,49]{3,1,2,0:T(8,128)S(1)}, f32[2,16,1,49]{3,1,2,0:T(8,128)S(1)}, u32[]{:S(2)}, u32[]{:S(2)}) collective-permute-start(f32[2,16,1,49]{3,1,2,0:T(8,128)S(1)} %pad_maximum_fusion.3), channel_id=1, source_target_pairs={{2,0},{4,2},{6,4},{8,6},{10,8},{12,10},{14,12},{16,14},{18,16},{20... | collective-permute-start | bytes 18824 | tf_op jit(solution)/shard_map/ppermute | solution.py:14
  15.1 8.2 %collective-permute-start.2 = (f32[2,1,9,49]{3,1,2,0:T(1,128)S(1)}, f32[2,1,9,49]{3,1,2,0:T(1,128)S(1)}, u32[]{:S(2)}, u32[]{:S(2)}) collective-permute-start(f32[2,1,9,49]{3,1,2,0:T(1,128)S(1)} %pad_maximum_fusion.4), channel_id=1, source_target_pairs={{32,0},{64,32},{96,64},{33,1},{65,33},{97,65},{34,2},{66,34},{98,6... | collective-permute-start | bytes 10592 | tf_op jit(solution)/shard_map/ppermute | solution.py:14
where the time goes:
time: 129 us; the launch traced here: 128 us
  Pallas kernels  90.1 us (70%)
  local copies, waits for them, and re-layouts  16.6 us (13%)
  waiting for transfers between devices  10.6 us (8%)
  starting transfers between devices  7.17 us (6%)
  other arithmetic  2.3 us (2%)
    pallas_call x1, Pallas kernels, reduced(): pl.pallas_call(functools.partial(reduce_kernel, cut), out_shape=[jax.Shap...  50.8 us
    pallas_call x1, Pallas kernels, per_device(): pl.pallas_call(functools.partial(kernel, 0.5 / total_cells), out_shape=ja...  39.4 us
    ppermute x3, waiting for transfers between devices, upper(): return lax.ppermute(head, axis, [(i + 1, i) for i in range(count - 1)])  10.6 us
    ppermute x3, starting transfers between devices, upper(): return lax.ppermute(head, axis, [(i + 1, i) for i in range(count - 1)])  7.17 us
    unnamed x13, local copies, waits for them, and re-layouts  4.18 us
    reshape x1, local copies, waits for them, and re-layouts, reduced(): part.reshape(nx, ny, nz, rows, wide)  2.84 us
  transfers between devices with their start and end apart: 3, of which 2 were waited for; matrix products, arithmetic and copies ran while one was open for 3% of the time, Pallas kernels for 0%

commit v1 on v0

--- a/solution.py
+++ b/solution.py
@@ -86,7 +86,7 @@
 
 def greet_around():
     barrier = pltpu.get_barrier_semaphore()
-    total = jnp.int32(0)
+    total = jnp.int32(greet_reduction())
     for offset in OFFSETS:
         for sign in (-1, 1):
             there = inside(offset, sign)
@@ -100,8 +100,8 @@
     pl.semaphore_wait(barrier, total)
 
 
-def kernel(scale, v_ref, z_ref, k_ref, t_ref, c_ref, out_ref, e_ref, corners, p0, p1, p2, p3, acc,
-           own_sem, send, recv, y_send, y_recv):
+def kernel(scale, v_ref, z_ref, k_ref, t_ref, c_ref, stiff_out, mass_out, e_ref, corners, p0, p1, p2, p3, acc,
+           own_sem, send, recv, y_send, y_recv, blocks, *reduce_bufs):
     slots = (p0, p1, p2, p3)
     rows, columns = e_ref.shape[1:]
     nx, owned, _ = v_ref.shape
@@ -204,9 +204,19 @@
     for x in range(4 * whole, planes):
         last = x == planes - 1
         step(x, x, 0.0 if last else 2.0, 0.0 if last else 4.0, x + 2 <= planes)
-    for half in range(2):
-        m = acc[:, half * columns:(half + 1) * columns]
-        out_ref[:, half * columns:(half + 1) * columns] = (m + m.T) * scale
+    groups = columns // 128
+    for g in range(groups):
+        some = slice(g * 128, (g + 1) * 128)
+        stiff = (acc[some, :columns] + acc[:, some].T) * scale
+        mass = (acc[some, columns:] + acc[:, columns + g * 128:columns + (g + 1) * 128].T) * scale
+        stiff = stiff.reshape(4, 4, 8, columns)
+        mass = mass.reshape(4, 4, 8, columns)
+        upper_rows = lax.broadcasted_iota(jnp.int32, stiff.shape, 2) < 4
+        low = jnp.where(upper_rows, stiff, pltpu.roll(mass, 4, 2))
+        high = jnp.where(upper_rows, pltpu.roll(stiff, 4, 2), mass)
+        blocks[g // 2, g % 2, :, :, 0] = low
+        blocks[g // 2, g % 2, :, :, 1] = high
+    reduce_blocks(blocks, stiff_out, mass_out, reduce_bufs)
     for i in range(nx // 4):
         pl.when(inside(y_here, -1))(chunk(i).wait_send)
     for offset in OFFSETS:
@@ -214,110 +224,106 @@
             pl.when(inside(offset, -1))(copies[offset].wait_send)
 
 
-def spread(axis, piece, landing, send, recv):
-    count = lax.axis_size(axis)
-    me = lax.axis_index(axis)
-    copies = []
+def coordinates():
+    gx, gy, gz = (lax.axis_index(a) for a in AXES)
+    return gx // 2, gx % 2, gy // 4, gy % 4, gz
+
+
+def places_along(axis):
+    zl, core, cx, cy, zh = coordinates()
+    count = 2 if axis == "core" else 4
+    me = {"core": core, "x": cx, "y": cy, "z": zh * 2 + zl}[axis]
+    found = []
     for k in range(1, count):
         peer = lax.rem(me + k, count)
+        if axis == "core":
+            device = {"gx": zl * 2 + peer}
+        elif axis == "x":
+            device = {"gy": peer * 4 + cy}
+        elif axis == "y":
+            device = {"gy": cx * 4 + peer}
+        else:
+            device = {"gx": (peer % 2) * 2 + core, "gz": peer // 2}
+        found.append((peer, device))
+    return found
+
+
+def greet_reduction():
+    barrier = pltpu.get_barrier_semaphore()
+    total = 0
+    for axis in ("core", "x", "y", "z"):
+        for _, device in places_along(axis):
+            pl.semaphore_signal(barrier, inc=1, device_id=device, device_id_type=pl.DeviceIdType.MESH)
+            total += 1
+    return total
+
+
+def spread(axis, piece, landing, send, recv, base):
+    copies = []
+    for k, (peer, device) in enumerate(places_along(axis)):
         copy = pltpu.make_async_remote_copy(
-            src_ref=piece(peer), dst_ref=landing.at[k - 1],
-            send_sem=send.at[k - 1], recv_sem=recv.at[k - 1],
-            device_id={axis: peer}, device_id_type=pl.DeviceIdType.MESH)
+            src_ref=piece(peer), dst_ref=landing.at[k],
+            send_sem=send.at[base + k], recv_sem=recv.at[base + k],
+            device_id=device, device_id_type=pl.DeviceIdType.MESH)
         copy.start()
         copies.append(copy)
     return copies
 
 
-def greet(axes):
-    barrier = pltpu.get_barrier_semaphore()
-    total = 0
-    for axis in axes:
-        count = lax.axis_size(axis)
-        me = lax.axis_index(axis)
-        for k in range(1, count):
-            pl.semaphore_signal(barrier, inc=1, device_id={axis: lax.rem(me + k, count)},
-                                device_id_type=pl.DeviceIdType.MESH)
-        total += count - 1
-    pl.semaphore_wait(barrier, total)
-
-
-def reduce_kernel(cut, part, stiff_out, mass_out, rz, sa, sb, ra1, rb1, ta, tb, ra2, rb2, out,
-                  *sems):
-    z_send, z_recv, a1s, a1r, b1s, b1r, a2s, a2r, b2s, b2r = sems
-    gx, gy, gz = (lax.axis_index(a) for a in ("gx", "gy", "gz"))
-    greet(("gx", "gy", "gz"))
-    first = spread("gz", lambda p: part.at[:, :, p], rz, z_send, z_recv)
-    for copy in first:
+def gathered(copies, own, landing):
+    for copy in copies:
         copy.wait_recv()
-    held = part[:, :, gz]
-    for k in range(len(first)):
-        held = held + rz[k]
-    sa[...] = held[..., :cut]
-    sb[...] = held[..., cut:]
-    a1 = spread("gy", lambda p: sa.at[:, p], ra1, a1s, a1r)
-    b1 = spread("gx", lambda p: sb.at[p], rb1, b1s, b1r)
-    for copy in a1:
-        copy.wait_recv()
-    held = sa[:, gy]
-    for k in range(len(a1)):
-        held = held + ra1[k]
-    ta[...] = held
-    a2 = spread("gx", lambda p: ta.at[p], ra2, a2s, a2r)
-    for copy in b1:
-        copy.wait_recv()
-    held = sb[gx]
-    for k in range(len(b1)):
-        held = held + rb1[k]
-    tb[...] = held
-    b2 = spread("gy", lambda p: tb.at[p], rb2, b2s, b2r)
-    for copy in a2:
-        copy.wait_recv()
-    held = ta[gx]
-    for k in range(len(a2)):
-        held = held + ra2[k]
-    out[:, :cut] = held
-    for copy in b2:
-        copy.wait_recv()
-    held = tb[gy]
-    for k in range(len(b2)):
-        held = held + rb2[k]
-    out[:, cut:] = held
-    columns = stiff_out.shape[1]
-    stiff_out[...] = out[:, :columns]
-    mass_out[...] = out[:, columns:]
-    for copy in first + a1 + b1 + a2 + b2:
+    held = own
+    for k in range(len(copies)):
+        held = held + landing[k]
+    return held
+
+
+def reduce_blocks(r, stiff_out, mass_out, bufs):
+    zl, core, cx, cy, zh = coordinates()
+    rc, ha, ra1, ha1, ra2, ha2, ra3, hb, rb1, hb1, rb2, hb2, rb3, send, recv = bufs
+    half = r.shape[-1] // 2
+    lanes = (slice(0, half), slice(half, 2 * half))
+    count = 0
+
+    def sems(n):
+        nonlocal count
+        count += n
+        return send, recv, count - n
+
+    first = [spread("core", lambda p, c=c: r.at[:, p, :, :, :, :, c], rc.at[i], *sems(1))
+             for i, c in enumerate(lanes)]
+    ha[...] = gathered(first[0], r[:, core, :, :, :, :, lanes[0]], rc.at[0])
+    a1 = spread("x", lambda p: ha.at[:, p], ra1, *sems(3))
+    hb[...] = gathered(first[1], r[:, core, :, :, :, :, lanes[1]], rc.at[1])
+    b1 = spread("z", lambda p: hb.at[p % 2, :, :, p // 2], rb1, *sems(3))
+    ha1[...] = gathered(a1, ha[:, cx], ra1)
+    a2 = spread("y", lambda p: ha1.at[:, p], ra2, *sems(3))
+    hb1[...] = gathered(b1, hb[zl, :, :, zh], rb1)
+    b2 = spread("x", lambda p: hb1.at[p], rb2, *sems(3))
+    ha2[...] = gathered(a2, ha1[:, cy], ra2)
+    a3 = spread("z", lambda p: ha2.at[p % 2, p // 2], ra3, *sems(3))
+    hb2[...] = gathered(b2, hb1[cx], rb2)
+    b3 = spread("y", lambda p: hb2.at[p], rb3, *sems(3))
+    done = gathered(a3, ha2[zl, zh], ra3)
+    stiff_out[:, :half] = done[:4]
+    mass_out[:, :half] = done[4:]
+    done = gathered(b3, hb2[cy], rb3)
+    stiff_out[:, half:] = done[:4]
+    mass_out[:, half:] = done[4:]
+    for copy in first[0] + first[1] + a1 + b1 + a2 + b2 + a3 + b3:
         copy.wait_send()
 
 
-def reduced(part):
-    nx, ny, nz = (lax.axis_size(a) for a in ("gx", "gy", "gz"))
-    wide = part.shape[1]
-    rows = part.shape[0] // (nx * ny * nz)
-    cut = (wide * 5 // 8) // 128 * 128
-    rest = wide - cut
+def reduce_scratch(columns):
+    half = columns // 2
     f32 = jnp.float32
-    dma = pltpu.SemaphoreType.DMA
-    vmem = pl.BlockSpec(memory_space=pltpu.VMEM)
-    return pl.pallas_call(
-        functools.partial(reduce_kernel, cut),
-        out_shape=[jax.ShapeDtypeStruct((rows, wide // 2), f32)] * 2,
-        in_specs=[vmem],
-        out_specs=[vmem, vmem],
-        scratch_shapes=[
-            pltpu.VMEM((nz - 1, nx, ny, rows, wide), f32),
-            pltpu.VMEM((nx, ny, rows, cut), f32),
-            pltpu.VMEM((nx, ny, rows, rest), f32),
-            pltpu.VMEM((ny - 1, nx, rows, cut), f32),
-            pltpu.VMEM((nx - 1, ny, rows, rest), f32),
-            pltpu.VMEM((nx, rows, cut), f32),
-            pltpu.VMEM((ny, rows, rest), f32),
-            pltpu.VMEM((nx - 1, rows, cut), f32),
-            pltpu.VMEM((ny - 1, rows, rest), f32),
-            pltpu.VMEM((rows, wide), f32),
-        ] + [dma((n - 1,)) for n in (nz, nz, ny, ny, nx, nx, nx, nx, ny, ny)],
-        compiler_params=pltpu.CompilerParams(collective_id=1, has_side_effects=True),
-    )(part.reshape(nx, ny, nz, rows, wide))
+    shapes = [(2, 1, 2, 4, 4, 2, 8, half),
+              (2, 4, 4, 2, 8, half), (3, 2, 4, 2, 8, half), (2, 4, 2, 8, half), (3, 2, 2, 8, half),
+              (2, 2, 8, half), (3, 8, half),
+              (2, 4, 4, 2, 8, half), (3, 4, 4, 8, half), (4, 4, 8, half), (3, 4, 8, half),
+              (4, 8, half), (3, 8, half)]
+    return [pltpu.VMEM(shape, f32) for shape in shapes] + [pltpu.SemaphoreType.DMA((20,))] * 2
 
 
 def per_device(eigvecs, material):
@@ -338,11 +344,11 @@
     matrix = jnp.asarray(plane_matrix(size_y, size_z, rows), jnp.bfloat16)
     vmem = pl.BlockSpec(memory_space=pltpu.VMEM)
     anywhere = pl.BlockSpec(memory_space=pl.ANY)
-    part = pl.pallas_call(
+    return tuple(pl.pallas_call(
         functools.partial(kernel, 0.5 / total_cells),
-        out_shape=jax.ShapeDtypeStruct((columns, 2 * columns), jnp.float32),
+        out_shape=[jax.ShapeDtypeStruct((4, columns), jnp.float32)] * 2,
         in_specs=[anywhere, vmem, vmem, vmem, vmem],
-        out_specs=vmem,
+        out_specs=[vmem, vmem],
         scratch_shapes=[
             pltpu.VMEM((size_x + 2, rows, columns), eigvecs.dtype),
             pltpu.VMEM((2, size_x, columns), eigvecs.dtype),
@@ -353,11 +359,11 @@
             pltpu.SemaphoreType.DMA((7,)),
             pltpu.SemaphoreType.DMA((size_x // 4,)),
             pltpu.SemaphoreType.DMA((size_x // 4,)),
-        ],
+            pltpu.VMEM((2, 2, 4, 4, 2, 8, columns), jnp.float32),
+        ] + reduce_scratch(columns),
         compiler_params=pltpu.CompilerParams(
             vmem_limit_bytes=60 * 1024 * 1024, collective_id=0, has_side_effects=True),
-    )(eigvecs.reshape(size_x, size_y * size_z, columns), z_layer, corner, matrix, coef)
-    return tuple(reduced(part))
+    )(eigvecs.reshape(size_x, size_y * size_z, columns), z_layer, corner, matrix, coef))
 
 
 def solution(mesh):

time: 129 us -> 98.1 us (0.76)
  Pallas kernels: 90.1 us -> 62.8 us
  local copies, waits for them, and re-layouts: 16.6 us -> 13.8 us
    pallas_call x2 -> x1, Pallas kernels: 90.1 us -> 62.8 us  [per_device(): pl.pallas_call(functools.partial(kernel, 0.5 / total_cells), out_shape=[j...]
    reshape x1 -> x0, local copies, waits for them, and re-layouts: 2.84 us -> none  [reduced(): part.reshape(nx, ny, nz, rows, wide)]
  transfers between devices with their start and end apart: 3 -> 3, of which waited for: 2 -> 2; matrix products, arithmetic and copies ran while one was open for 3% -> 4% of each run, Pallas kernels for 0% -> 0%
where the time goes in v1:
time: 98.1 us; the launch traced here: 97.5 us
  Pallas kernels  62.8 us (64%)
  local copies, waits for them, and re-layouts  13.8 us (14%)
  waiting for transfers between devices  10.6 us (11%)
  starting transfers between devices  7.17 us (7%)
  other arithmetic  2.3 us (2%)
    pallas_call x1, Pallas kernels, per_device(): pl.pallas_call(functools.partial(kernel, 0.5 / total_cells), out_shape=[j...  62.8 us
    ppermute x3, waiting for transfers between devices, upper(): return lax.ppermute(head, axis, [(i + 1, i) for i in range(count - 1)])  10.6 us
    ppermute x3, starting transfers between devices, upper(): return lax.ppermute(head, axis, [(i + 1, i) for i in range(count - 1)])  7.17 us
    unnamed x13, local copies, waits for them, and re-layouts  4.19 us
    reshape x2, local copies, waits for them, and re-layouts, coefficients(): main = parts[..., :size_z].reshape(size_x + 1, 3, (size_y + 1) * size_z)  2.22 us
  transfers between devices with their start and end apart: 3, of which 2 were waited for; matrix products, arithmetic and copies ran while one was open for 4% of the time, Pallas kernels for 0%

profile of v1, /device:TPU:1, one launch (start us, length us, event | category | flops | bytes accessed | tf_op | source)
XLA Modules:
  0.0 97.5 jit_solution(4128613154077174599)
XLA Ops:
  0.6 0.9 copy.68
  1.6 1.4 %collective-permute-start = (f32[2,16,8,1]{3,1,2,0:T(8,128)S(1)}, f32[2,16,8,1]{3,1,2,0:T(8,128)S(1)}, u32[]{:S(2)}, u32[]{:S(2)}) collective-permute-start(f32[2,16,8,1]{3,1,2,0:T(8,128)S(1)} %bitcast.22), channel_id=1, source_target_pairs={{1,0},{3,2},{5,4},{7,6},{9,8},{11,10},{13,12},{15,14},{17,16},{19,... | collective-permute-start | bytes 3080 | tf_op jit(solution)/shard_map/ppermute | solution.py:14
  3.1 7.4 %collective-permute-done = f32[2,16,8,1]{3,1,2,0:T(8,128)S(1)} collective-permute-done((f32[2,16,8,1]{3,1,2,0:T(8,128)S(1)}, f32[2,16,8,1]{3,1,2,0:T(8,128)S(1)}, u32[]{:S(2)}, u32[]{:S(2)}) %collective-permute-start) | collective-permute-done | bytes 1056 | tf_op jit(solution)/shard_map/ppermute | solution.py:14
  10.6 1.3 %collective-permute-start.1 = (f32[2,16,1,49]{3,1,2,0:T(8,128)S(1)}, f32[2,16,1,49]{3,1,2,0:T(8,128)S(1)}, u32[]{:S(2)}, u32[]{:S(2)}) collective-permute-start(f32[2,16,1,49]{3,1,2,0:T(8,128)S(1)} %pad_maximum_fusion.3), channel_id=1, source_target_pairs={{2,0},{4,2},{6,4},{8,6},{10,8},{12,10},{14,12},{16,14},{18,16},{20... | collective-permute-start | bytes 18824 | tf_op jit(solution)/shard_map/ppermute | solution.py:14
  11.8 3.2 %collective-permute-done.1 = f32[2,16,1,49]{3,1,2,0:T(8,128)S(1)} collective-permute-done((f32[2,16,1,49]{3,1,2,0:T(8,128)S(1)}, f32[2,16,1,49]{3,1,2,0:T(8,128)S(1)}, u32[]{:S(2)}, u32[]{:S(2)}) %collective-permute-start.1) | collective-permute-done | bytes 6304 | tf_op jit(solution)/shard_map/ppermute | solution.py:14
  15.1 4.5 %collective-permute-start.2 = (f32[2,1,9,49]{3,1,2,0:T(1,128)S(1)}, f32[2,1,9,49]{3,1,2,0:T(1,128)S(1)}, u32[]{:S(2)}, u32[]{:S(2)}) collective-permute-start(f32[2,1,9,49]{3,1,2,0:T(1,128)S(1)} %pad_maximum_fusion.4), channel_id=1, source_target_pairs={{32,0},{64,32},{96,64},{33,1},{65,33},{97,65},{34,2},{66,34},{98,6... | collective-permute-start | bytes 10592 | tf_op jit(solution)/shard_map/ppermute | solution.py:14
  19.6 0.9 slice.49
  20.5 1.4 %slice.48 = bf16[16,8,1,512]{3,2,1,0:T(2,128)(2,1)S(1)} slice(bf16[16,8,48,512]{3,2,1,0:T(8,128)(2,1)} %param.7), slice={[0:16], [0:8], [0:1], [0:512]} | slice | bytes 262144 | tf_op jit(solution)/shard_map/slice | solution.py:342
  21.9 0.6 copy.89
  22.6 0.7 pad.24.z_ref
  23.7 0.1 add_bitcast_fusion
  23.8 0.6 copy.71
  24.4 0.6 copy.72
  25.0 0.6 copy.73
  25.7 0.1 pad_maximum_fusion.2
  25.8 1.5 %pad_maximum_fusion = f32[17,3,9,49]{2,1,0,3:T(4,128)S(1)} fusion(f32[17,1,9,49]{2,1,0,3:T(1,128)S(1)} %copy.73, f32[17,1,9,49]{2,1,0,3:T(1,128)S(1)} %copy.72, f32[17,1,9,49]{2,1,0,3:T(1,128)S(1)} %copy.71), kind=kLoop, calls=%fused_computation | loop fusion | flops 44982 | bytes 179928 | tf_op jit(solution)/shard_map/stack | solution.py:61
  27.4 0.1 copy.77
  27.5 1.5 %slice.67 = f32[17,3,9,48]{2,1,0,3:T(4,128)} slice(f32[17,3,9,49]{2,1,0,3:T(4,128)S(1)} %pad_maximum_fusion), slice={[0:17], [0:3], [0:9], [0:48]} | slice | bytes 176256 | tf_op jit(solution)/shard_map/slice | solution.py:62
  29.0 2.0 %copy.82 = f32[17,3,9,48]{3,2,1,0:T(8,128)S(1)} copy(f32[17,3,9,48]{2,1,0,3:T(4,128)} %slice.67) | data formatting | bytes 176256 | tf_op jit(solution)/shard_map/reshape | solution.py:62
  31.1 0.2 reshape.36
  31.4 0.7 pad.29.c_ref
  32.1 62.8 %shard_map.86 = (f32[4,512]{1,0:T(4,128)}, f32[4,512]{1,0:T(4,128)}) custom-call(bf16[16,384,512]{2,1,0:T(8,128)(2,1)} %bitcast.21, bf16[16,16,512]{2,1,0:T(8,128)(2,1)} %pad.24.z_ref, bf16[16,512]{1,0:T(8,128)(2,1)} %bitcast.24, bf16[928,464]{1,0:T(8,128)(2,1)} %constant.25.clone.t_ref, f32[17,8,464]{2,1,0:T(8,128)} %pad.29.c_ref), custom_call_target="tpu_custom_call" | custom-call | tf_op jit(solution)/shard_map/pallas_call | solution.py:347
  95.0 1.3 %copy.92 = f32[4,512]{1,0:T(4,128)} copy(f32[4,512]{1,0:T(4,128)} %get-tuple-element.7) | data formatting | bytes 16384
  96.2 1.3 %copy.93 = f32[4,512]{1,0:T(4,128)} copy(f32[4,512]{1,0:T(4,128)} %get-tuple-element.8) | data formatting | bytes 16384
  (19 shorter events, 0.7 us)
Async XLA Ops:
  0.6 22.8 %copy-start.2 = (f32[17]{0:T(128)S(1)}, f32[17]{0:T(128)}, u32[]{:S(2)}) copy-start(f32[17]{0:T(128)} %constant.40) | copy-start | bytes 208
  1.6 22.0 %copy-start.1 = (f32[9]{0:T(128)S(1)}, f32[9]{0:T(128)}, u32[]{:S(2)}) copy-start(f32[9]{0:T(128)} %constant.41) | copy-start | bytes 112
  1.6 22.1 %copy-start = (f32[17,9,49]{2,0,1:T(8,128)S(1)}, f32[17,9,49]{2,0,1:T(8,128)}, u32[]{:S(2)}) copy-start(f32[17,9,49]{2,0,1:T(8,128)} %constant.24.clone) | copy-start | bytes 89968
  1.6 22.1 %copy-start.3 = (f32[49]{0:T(128)S(1)}, f32[49]{0:T(128)}, u32[]{:S(2)}) copy-start(f32[49]{0:T(128)} %constant.42) | copy-start | bytes 592
  1.6 8.9 %collective-permute-start = (f32[2,16,8,1]{3,1,2,0:T(8,128)S(1)}, f32[2,16,8,1]{3,1,2,0:T(8,128)S(1)}, u32[]{:S(2)}, u32[]{:S(2)}) collective-permute-start(f32[2,16,8,1]{3,1,2,0:T(8,128)S(1)} %bitcast.22), channel_id=1, source_target_pairs={{1,0},{3,2},{5,4},{7,6},{9,8},{11,10},{13,12},{15,14},{17,16},{19,... | collective-permute-start | bytes 3080 | tf_op jit(solution)/shard_map/ppermute | solution.py:14
  10.6 4.5 %collective-permute-start.1 = (f32[2,16,1,49]{3,1,2,0:T(8,128)S(1)}, f32[2,16,1,49]{3,1,2,0:T(8,128)S(1)}, u32[]{:S(2)}, u32[]{:S(2)}) collective-permute-start(f32[2,16,1,49]{3,1,2,0:T(8,128)S(1)} %pad_maximum_fusion.3), channel_id=1, source_target_pairs={{2,0},{4,2},{6,4},{8,6},{10,8},{12,10},{14,12},{16,14},{18,16},{20... | collective-permute-start | bytes 18824 | tf_op jit(solution)/shard_map/ppermute | solution.py:14
  15.1 8.2 %collective-permute-start.2 = (f32[2,1,9,49]{3,1,2,0:T(1,128)S(1)}, f32[2,1,9,49]{3,1,2,0:T(1,128)S(1)}, u32[]{:S(2)}, u32[]{:S(2)}) collective-permute-start(f32[2,1,9,49]{3,1,2,0:T(1,128)S(1)} %pad_maximum_fusion.4), channel_id=1, source_target_pairs={{32,0},{64,32},{96,64},{33,1},{65,33},{97,65},{34,2},{66,34},{98,6... | collective-permute-start | bytes 10592 | tf_op jit(solution)/shard_map/ppermute | solution.py:14

commit v2 on v1

v2 whole, which is shorter than its diff:
```python
import functools
import numpy as np
import jax
import jax.numpy as jnp
from jax import lax
from jax.experimental import pallas as pl
from jax.experimental.pallas import tpu as pltpu
from jax.sharding import PartitionSpec as P

AXES = ("gx", "gy", "gz")
MESH = pl.DeviceIdType.MESH
NEAR = [(a, b, c) for c in (0, 1) for a in (-1, 0, 1) for b in (-1, 0, 1) if (a, b, c) != (0, 0, 0)]
STEP = 2


def weight(distance, middle):
    return {0: middle, 1: 1.0}.get(abs(distance), 0.0)


def own_row(y, size_y, size_z):
    half = size_y // 2
    if y < half:
        return size_z * (y + 1)
    return size_z * (half + 1) + 16 + size_z * (y - half)


def plane_taps(size_y, size_z):
    half = size_y // 2
    block = size_z * (half + 1) + 16
    taps = np.zeros((2, 2, size_y * size_z, 2 * block), np.float32)
    for side in range(2):
        edge = size_z - 1 if side == 0 else 0
        for n, middle in enumerate((2.0, 4.0)):
            line = np.array([[weight(z - o, middle) for z in range(size_z)] for o in range(size_z)])
            for y in range(size_y):
                rows = slice(y * size_z, (y + 1) * size_z)
                for near in (y - 1, y, y + 1):
                    w = weight(near - y, middle)
                    if near < 0:
                        first = 0
                    else:
                        first = own_row(near, size_y, size_z)
                    taps[side, n, rows, first:first + size_z] = w * line
                    column = near if 0 <= near < size_y else (size_y if near < 0 else size_y + 1)
                    base = (block if near < half else 2 * block) - 16
                    taps[side, n, y * size_z + edge, base + column] = w
    return taps


def material_taps(size_x, size_y):
    cells = size_x * size_y
    places = [(x, y) for x in range(size_x) for y in range(size_y)]
    places += [(x, y) for x in (-1, size_x) for y in range(size_y)]
    places += [(x, y) for y in (-1, size_y) for x in range(size_x)]
    for x in (-1, size_x):
        for y in (-1, size_y):
            places += [(x, y) if n == (7 if x < 0 else 0) else None for n in range(8)]
    rows = -(-len(places) // 128) * 128
    taps = np.zeros((rows, cells), np.float32)
    for row, place in enumerate(places):
        if place is None:
            continue
        for x in range(size_x):
            for y in range(size_y):
                taps[row, x * size_y + y] = weight(x - place[0], 2.0) * weight(y - place[1], 2.0)
    return taps


def inside(a, b):
    gx, gy = lax.axis_index("gx"), lax.axis_index("gy")
    ok = None
    for at, d, count in ((gx, a, lax.axis_size("gx")), (gy, b, lax.axis_size("gy"))):
        if d:
            here = at > 0 if d < 0 else at < count - 1
            ok = here if ok is None else jnp.logical_and(ok, here)
    return ok


def when(condition):
    return (lambda f: f()) if condition is None else pl.when(condition)


def device_at(a, b, c):
    device = {}
    if a:
        device["gx"] = lax.axis_index("gx") + a
    if b:
        device["gy"] = lax.axis_index("gy") + b
    if c:
        device["gz"] = 1 - lax.axis_index("gz")
    return device


def greet_around():
    barrier = pltpu.get_barrier_semaphore()
    total = jnp.int32(greet_reduction())
    for a, b, c in NEAR:
        there = inside(a, b)

        @when(there)
        def _(a=a, b=b, c=c):
            pl.semaphore_signal(barrier, inc=1, device_id=device_at(a, b, c), device_id_type=MESH)

        total = total + (1 if there is None else jnp.where(there, 1, 0))
    return total


class Halo:
    def __init__(self, send, recv):
        self.send, self.recv, self.count, self.all = send, recv, 0, []

    def add(self, side, src, dst):
        a, b, c = side
        copy = pltpu.make_async_remote_copy(
            src_ref=src, dst_ref=dst, send_sem=self.send.at[self.count], recv_sem=self.recv.at[self.count],
            device_id=device_at(-a, -b, c), device_id_type=MESH)
        self.count += 1
        entry = (copy, inside(-a, -b), inside(a, b))
        self.all.append(entry)
        return entry

    def finish(self):
        for copy, sends, _ in self.all:
            when(sends)(copy.wait_send)


def begin(entries):
    for copy, sends, _ in entries:
        when(sends)(copy.start)


def arrive(entries):
    for copy, _, receives in entries:
        when(receives)(copy.wait_recv)


def zero_unless(condition, refs):
    if condition is None:
        return

    @pl.when(jnp.logical_not(condition))
    def _():
        for ref in refs:
            ref[...] = jnp.zeros(ref.shape, ref.dtype)


def kernel(scale, sizes, v_ref, m_ref, t_hbm, w_ref, stiff_out, mass_out,
           e, t, zl, zn, cz, cn, zx, cx, faces, kall, coef, u, ybuf, acc, blocks,
           own_sem, v_send, v_recv, k_send, k_recv, *reduce_bufs):
    nx, ny, nz = sizes
    columns = e.shape[2]
    gz = lax.axis_index("gz")
    hy = ny // 2 * nz
    block = nz + hy + 16
    cells = nx * ny
    low, high = pl.ds(nz, hy), pl.ds(block, hy)
    own = [pltpu.make_async_copy(v_ref.at[:, :hy], e.at[pl.ds(1, nx), low], own_sem.at[0]),
           pltpu.make_async_copy(v_ref.at[:, hy:], e.at[pl.ds(1, nx), high], own_sem.at[1]),
           pltpu.make_async_copy(t_hbm.at[gz], t, own_sem.at[2])]
    for copy in own:
        copy.start()
    total = greet_around()

    kappa = m_ref[0]
    for n, y in enumerate((0, ny - 1)):
        faces[n] = jnp.concatenate([kappa[x * ny + y:x * ny + y + 1] for x in range(nx)], 0)
    kall[0, :cells] = kappa

    row = lax.broadcasted_iota(jnp.int32, (nz, nz), 0)
    col = lax.broadcasted_iota(jnp.int32, (nz, nz), 1)
    exact = functools.partial(lax.dot_general, dimension_numbers=(((1,), (1,)), ((), ())),
                              precision=lax.Precision.HIGHEST, preferred_element_type=jnp.float32)
    unit = jnp.where(row == col, 1.0, 0.0)

    def fill_coefficients(n, field):
        for x in range(nx):
            for y in range(ny):
                at = x * ny + y
                coef[n, x, y * nz:(y + 1) * nz] = jnp.broadcast_to(field[:, at:at + 1], (nz, 128))

    flipped = exact(unit, kappa)
    fill_coefficients(1, flipped * (1.0 / 16.0))
    fill_coefficients(2, exact(unit, m_ref[1]) * (1.0 / 216.0))

    pl.semaphore_wait(pltpu.get_barrier_semaphore(), total)

    kh = Halo(k_send, k_recv)
    x_tile = {-1: pl.ds(cells - ny, ny), 1: pl.ds(0, ny)}
    f_tile = {-1: pl.ds(nx - 8, 8), 1: pl.ds(0, 8)}
    which = {-1: 0, 1: 1}
    y_face = {-1: 1, 1: 0}
    for a, b, c in NEAR:
        if (a, b) == (0, 0):
            src, at, n = m_ref.at[0], 0, cells
        elif b == 0:
            src, at, n = m_ref.at[0, x_tile[a]], cells + which[a] * ny, ny
        elif a == 0:
            src, at, n = faces.at[y_face[b]], cells + 2 * ny + which[b] * nx, nx
        else:
            src = faces.at[y_face[b], f_tile[a]]
            at, n = cells + 2 * ny + 2 * nx + 8 * (2 * which[a] + which[b]), 8
        dst = kall.at[c, pl.ds(at, n)]
        begin([kh.add((a, b, c), src, dst)])
        zero_unless(inside(a, b), [dst])
    used = cells + 2 * ny + 2 * nx + 32
    for c in range(2):
        kall[c, used:] = jnp.zeros((kall.shape[1] - used, nz), jnp.float32)

    vh = Halo(v_send, v_recv)
    steps = nx // STEP
    waits = [[] for _ in range(steps)]
    y_src = {-1: pl.ds((ny - 1) * nz, nz), 1: pl.ds(0, nz)}
    y_dst = {-1: pl.ds(0, nz), 1: pl.ds(block + hy, nz)}
    x_src = {-1: nx - 1, 1: 0}
    x_dst = {-1: 0, 1: nx + 1}

    def y_chunk(i):
        first = 0 if i == 0 else STEP * i + 1
        last = min(STEP * (i + 1) + 1, nx)
        made = [vh.add((0, b, 0), v_ref.at[pl.ds(first, last - first), y_src[b]],
                       e.at[pl.ds(first + 1, last - first), y_dst[b]]) for b in (-1, 1)]
        waits[i].extend(made)
        begin(made)

    def x_plane(a):
        made = [vh.add((a, 0, 0), v_ref.at[x_src[a], pl.ds(0, hy)], e.at[x_dst[a], low]),
                vh.add((a, 0, 0), v_ref.at[x_src[a], pl.ds(hy, hy)], e.at[x_dst[a], high])]
        made += [vh.add((a, b, 0), v_ref.at[x_src[a], y_src[b]], e.at[x_dst[a], y_dst[b]]) for b in (-1, 1)]
        waits[0 if a < 0 else steps - 1].extend(made)
        begin(made)

    y_chunk(0)
    x_plane(-1)
    for i in range(1, steps):
        y_chunk(i)
    for b in (-1, 1):
        zero_unless(inside(0, b), [e.at[pl.ds(1, nx), y_dst[b]]])
    for a in (-1, 1):
        zero_unless(inside(a, 0), [e.at[x_dst[a], low], e.at[x_dst[a], high], zx.at[which[a]]])
        for b in (-1, 1):
            zero_unless(inside(a, b), [e.at[x_dst[a], y_dst[b]], cx.at[which[a], which[b]]])
    for b in (-1, 1):
        zero_unless(inside(0, b), [cn.at[which[b]]])
    acc[...] = jnp.zeros_like(acc)

    own[0].wait()
    own[1].wait()

    def edge_row(x, y, z):
        at = own_row(y, ny, nz) + z
        first = at // 16 * 16
        return e[x + 1, first:first + 16].astype(jnp.float32)[at - first:at - first + 1]

    def extract(z):
        for q in range(nx // 2):
            rows = [edge_row(2 * q + n // ny, n % ny, z) for n in range(2 * ny)]
            zl[q] = jnp.concatenate(rows, 0).astype(zl.dtype)
        for n, y in enumerate((0, ny - 1)):
            cz[n] = jnp.concatenate([edge_row(x, y, z) for x in range(nx)], 0).astype(cz.dtype)

    pl.when(gz == 0)(functools.partial(extract, nz - 1))
    pl.when(gz == 1)(functools.partial(extract, 0))

    def z_chunk(i):
        first, last = (0, 2) if i == 0 else (i + 1, i + 2)
        made = [vh.add((0, 0, 1), zl.at[pl.ds(first, last - first)], zn.at[pl.ds(first, last - first)])]
        waits[i].extend(made)
        begin(made)

    def z_corners(a):
        if a == 0:
            made = [vh.add((0, b, 1), cz.at[y_face[b]], cn.at[which[b]]) for b in (-1, 1)]
        else:
            made = [vh.add((a, 0, 1), zl.at[nx // 2 - 1 if a < 0 else 0], zx.at[which[a]])]
            made += [vh.add((a, b, 1), cz.at[y_face[b]], cx.at[which[a], which[b]]) for b in (-1, 1)]
        waits[0 if a <= 0 else steps - 1].extend(made)
        begin(made)

    z_chunk(0)
    z_corners(0)
    z_corners(-1)
    for i in range(1, steps - 1):
        z_chunk(i)
    z_corners(1)
    x_plane(1)

    arrive(kh.all)
    edge_from = jnp.where(gz == 0, nz - 1, 0)
    near_z = jnp.where(jnp.abs(row - col) == 1, 1.0, 0.0) + 2.0 * unit
    across = jnp.where(jnp.logical_and(row == edge_from, col == nz - 1 - edge_from), 1.0, 0.0)
    along_z = exact(near_z, kall[0]) + exact(across, kall[1])
    field = lax.dot_general(along_z, w_ref[...], (((1,), (0,)), ((), ())),
                            precision=lax.Precision.HIGHEST, preferred_element_type=jnp.float32)
    fill_coefficients(0, 2.0 * flipped + (1.0 / 32.0) * field)
    own[2].wait()

    lane = lax.broadcasted_iota(jnp.int32, (8, columns), 0)

    def fill_edge(x):
        if x < 0:
            z8 = zx[0].astype(jnp.float32)[8:]
            corners = [cx[0, n].astype(jnp.float32)[nx - 1:] for n in range(2)]
        elif x == nx:
            z8 = zx[1].astype(jnp.float32)[:8]
            corners = [cx[1, n].astype(jnp.float32)[:1] for n in range(2)]
        else:
            z8 = zn[x // 2].astype(jnp.float32)[8 * (x % 2):8 * (x % 2) + 8]
            corners = [cn[n].astype(jnp.float32)[x:x + 1] for n in range(2)]
        c8 = jnp.where(lane == 0, corners[0], jnp.where(lane == 1, corners[1], 0.0))
        full = jnp.concatenate([z8, c8], 0).astype(e.dtype)
        e[x + 1, block - 16:block] = full
        e[x + 1, 2 * block - 16:] = full

    def taps_of(n, slot):
        cut = hy - nz
        one = jnp.dot(t[n, :cut, :block], u[slot, n, :block], preferred_element_type=jnp.float32)
        two = jnp.dot(t[n, cut:cut + 2 * nz], u[slot, n], preferred_element_type=jnp.float32)
        three = jnp.dot(t[n, cut + 2 * nz:, block:], u[slot, n, block:], preferred_element_type=jnp.float32)
        return jnp.concatenate([one, two, three], 0)

    def spread_lanes(c):
        return jnp.concatenate([c] * (columns // 128), 1)

    def iteration(i, carry):
        for c in range(steps):
            @pl.when(i == c)
            def _(c=c):
                arrive(waits[c])
                first = -1 if c == 0 else STEP * c + 1
                for x in range(first, STEP * (c + 1) + 1):
                    fill_edge(x)

        held = []
        for j in range(STEP):
            x = STEP * i + j
            here = e[x + 1]
            twice = here + here
            two = e[x] + e[x + 2] + twice
            u[j, 0] = two
            u[j, 1] = two + twice
            v = jnp.concatenate([here[nz:nz + hy], here[block:block + hy]], 0)
            held.append(v)
            rows = slice(j * ny * nz, (j + 1) * ny * nz)
            stiff = spread_lanes(coef[0, x]) * v.astype(jnp.float32) - spread_lanes(coef[1, x]) * taps_of(0, j)
            ybuf[rows, :columns] = stiff.astype(ybuf.dtype)
            mass = spread_lanes(coef[2, x]) * taps_of(1, j)
            ybuf[rows, columns:] = mass.astype(ybuf.dtype)
        acc[...] += lax.dot_general(jnp.concatenate(held, 0), ybuf[...], (((0,), (0,)), ((), ())),
                                    preferred_element_type=jnp.float32)
        return carry

    lax.fori_loop(0, steps, iteration, 0)

    for g in range(columns // 128):
        some = slice(g * 128, (g + 1) * 128)
        stiff = (acc[some, :columns] + acc[:, some].T) * scale
        mass = (acc[some, columns:] + acc[:, columns + g * 128:columns + (g + 1) * 128].T) * scale
        stiff = stiff.reshape(4, 4, 8, columns)
        mass = mass.reshape(4, 4, 8, columns)
        upper_rows = lax.broadcasted_iota(jnp.int32, stiff.shape, 2) < 4
        blocks[g // 2, g % 2, :, :, 0] = jnp.where(upper_rows, stiff, pltpu.roll(mass, 4, 2))
        blocks[g // 2, g % 2, :, :, 1] = jnp.where(upper_rows, pltpu.roll(stiff, 4, 2), mass)
    reduce_blocks(blocks, stiff_out, mass_out, reduce_bufs)
    kh.finish()
    vh.finish()


def coordinates():
    gx, gy, gz = (lax.axis_index(a) for a in AXES)
    return gx // 2, gx % 2, gy // 4, gy % 4, gz


def places_along(axis):
    zl, core, cx, cy, zh = coordinates()
    count = 2 if axis == "core" else 4
    me = {"core": core, "x": cx, "y": cy, "z": zh * 2 + zl}[axis]
    found = []
    for k in range(1, count):
        peer = lax.rem(me + k, count)
        if axis == "core":
            device = {"gx": zl * 2 + peer}
        elif axis == "x":
            device = {"gy": peer * 4 + cy}
        elif axis == "y":
            device = {"gy": cx * 4 + peer}
        else:
            device = {"gx": (peer % 2) * 2 + core, "gz": peer // 2}
        found.append((peer, device))
    return found


def greet_reduction():
    barrier = pltpu.get_barrier_semaphore()
    total = 0
    for axis in ("core", "x", "y", "z"):
        for _, device in places_along(axis):
            pl.semaphore_signal(barrier, inc=1, device_id=device, device_id_type=pl.DeviceIdType.MESH)
            total += 1
    return total


def spread(axis, piece, landing, send, recv, base):
    copies = []
    for k, (peer, device) in enumerate(places_along(axis)):
        copy = pltpu.make_async_remote_copy(
            src_ref=piece(peer), dst_ref=landing.at[k],
            send_sem=send.at[base + k], recv_sem=recv.at[base + k],
            device_id=device, device_id_type=pl.DeviceIdType.MESH)
        copy.start()
        copies.append(copy)
    return copies


def gathered(copies, own, landing):
    for copy in copies:
        copy.wait_recv()
    held = own
    for k in range(len(copies)):
        held = held + landing[k]
    return held


def reduce_blocks(r, stiff_out, mass_out, bufs):
    zl, core, cx, cy, zh = coordinates()
    rc, ha, ra1, ha1, ra2, ha2, ra3, hb, rb1, hb1, rb2, hb2, rb3, send, recv = bufs
    half = r.shape[-1] // 2
    lanes = (slice(0, half), slice(half, 2 * half))
    count = 0

    def sems(n):
        nonlocal count
        count += n
        return send, recv, count - n

    first = [spread("core", lambda p, c=c: r.at[:, p, :, :, :, :, c], rc.at[i], *sems(1))
             for i, c in enumerate(lanes)]
    ha[...] = gathered(first[0], r[:, core, :, :, :, :, lanes[0]], rc.at[0])
    a1 = spread("x", lambda p: ha.at[:, p], ra1, *sems(3))
    hb[...] = gathered(first[1], r[:, core, :, :, :, :, lanes[1]], rc.at[1])
    b1 = spread("z", lambda p: hb.at[p % 2, :, :, p // 2], rb1, *sems(3))
    ha1[...] = gathered(a1, ha[:, cx], ra1)
    a2 = spread("y", lambda p: ha1.at[:, p], ra2, *sems(3))
    hb1[...] = gathered(b1, hb[zl, :, :, zh], rb1)
    b2 = spread("x", lambda p: hb1.at[p], rb2, *sems(3))
    ha2[...] = gathered(a2, ha1[:, cy], ra2)
    a3 = spread("z", lambda p: ha2.at[p % 2, p // 2], ra3, *sems(3))
    hb2[...] = gathered(b2, hb1[cx], rb2)
    b3 = spread("y", lambda p: hb2.at[p], rb3, *sems(3))
    done = gathered(a3, ha2[zl, zh], ra3)
    stiff_out[:, :half] = done[:4]
    mass_out[:, :half] = done[4:]
    done = gathered(b3, hb2[cy], rb3)
    stiff_out[:, half:] = done[:4]
    mass_out[:, half:] = done[4:]
    for copy in first[0] + first[1] + a1 + b1 + a2 + b2 + a3 + b3:
        copy.wait_send()


def reduce_scratch(columns):
    half = columns // 2
    f32 = jnp.float32
    shapes = [(2, 1, 2, 4, 4, 2, 8, half),
              (2, 4, 4, 2, 8, half), (3, 2, 4, 2, 8, half), (2, 4, 2, 8, half), (3, 2, 2, 8, half),
              (2, 2, 8, half), (3, 8, half),
              (2, 4, 4, 2, 8, half), (3, 4, 4, 8, half), (4, 4, 8, half), (3, 4, 8, half),
              (4, 8, half), (3, 8, half)]
    return [pltpu.VMEM(shape, f32) for shape in shapes] + [pltpu.SemaphoreType.DMA((20,))] * 2


def per_device(eigvecs, material):
    nx, ny, nz, columns = eigvecs.shape
    total_cells = nx * ny * nz
    for axis in AXES:
        total_cells *= lax.axis_size(axis)
    hy = ny // 2 * nz
    block = nz + hy + 16
    cells = nx * ny
    taps = jnp.asarray(plane_taps(ny, nz), jnp.bfloat16)
    around = jnp.asarray(material_taps(nx, ny), jnp.float32)
    bf16, f32 = jnp.bfloat16, jnp.float32
    dma = pltpu.SemaphoreType.DMA
    vmem = pl.BlockSpec(memory_space=pltpu.VMEM)
    anywhere = pl.BlockSpec(memory_space=pl.ANY)
    scratch = [
        pltpu.VMEM((nx + 2, 2 * block, columns), bf16),
        pltpu.VMEM((2, ny * nz, 2 * block), bf16),
        pltpu.VMEM((nx // 2, 2 * ny, columns), bf16),
        pltpu.VMEM((nx // 2, 2 * ny, columns), bf16),
        pltpu.VMEM((2, nx, columns), bf16),
        pltpu.VMEM((2, nx, columns), bf16),
        pltpu.VMEM((2, 2 * ny, columns), bf16),
        pltpu.VMEM((2, 2, nx, columns), bf16),
        pltpu.VMEM((2, nx, nz), f32),
        pltpu.VMEM((2, around.shape[0], nz), f32),
        pltpu.VMEM((3, nx, ny * nz, 128), f32),
        pltpu.VMEM((STEP, 2, 2 * block, columns), bf16),
        pltpu.VMEM((STEP * ny * nz, 2 * columns), bf16),
        pltpu.VMEM((columns, 2 * columns), f32),
        pltpu.VMEM((2, 2, 4, 4, 2, 8, columns), f32),
        dma((3,)), dma((48,)), dma((48,)), dma((17,)), dma((17,)),
    ] + reduce_scratch(columns)
    return tuple(pl.pallas_call(
        functools.partial(kernel, 0.5 / total_cells, (nx, ny, nz)),
        out_shape=[jax.ShapeDtypeStruct((4, columns), f32)] * 2,
        in_specs=[anywhere, vmem, anywhere, vmem],
        out_specs=[vmem, vmem],
        scratch_shapes=scratch,
        compiler_params=pltpu.CompilerParams(
            vmem_limit_bytes=60 * 1024 * 1024, collective_id=0, has_side_effects=True),
    )(eigvecs.reshape(nx, ny * nz, columns), material.reshape(2, cells, nz), taps, around))


def solution(mesh):
    return jax.shard_map(
        per_device,
        mesh=mesh,
        in_specs=(P("gx", "gy", "gz", None), P(None, "gx", "gy", "gz")),
        out_specs=(P(("gx", "gy", "gz"), None), P(("gx", "gy", "gz"), None)),
        check_vma=False,
    )
```

time: 98.1 us -> 72.9 us (0.74)
  local copies, waits for them, and re-layouts: 13.8 us -> 2.59 us
  waiting for transfers between devices: 10.6 us -> 0 us
  starting transfers between devices: 7.17 us -> 0 us
  Pallas kernels: 62.8 us -> 68.3 us
  other arithmetic: 2.3 us -> 0 us
    ppermute x3 -> x0, waiting for transfers between devices: 10.6 us -> none  [upper(): return lax.ppermute(head, axis, [(i + 1, i) for i in range(count - 1)])]
    ppermute x3 -> x0, starting transfers between devices: 7.17 us -> none  [upper(): return lax.ppermute(head, axis, [(i + 1, i) for i in range(count - 1)])]
    pallas_call x1, Pallas kernels: 62.8 us -> 68.3 us  [per_device(): pl.pallas_call(functools.partial(kernel, 0.5 / total_cells, (nx, ny, nz))...]
    slice x4 -> x0, local copies, waits for them, and re-layouts: 3.93 us -> none  [the longest x1 1.49 us: coefficients(): main = parts[..., :size_z].reshape(size_x + 1, 3, (size_y + 1) * size_z)]
    reshape x2 -> x0, local copies, waits for them, and re-layouts: 2.22 us -> none  [coefficients(): main = parts[..., :size_z].reshape(size_x + 1, 3, (size_y + 1) * size_z)]
    unnamed x13 -> x2, local copies, waits for them, and re-layouts: 4.19 us -> 2.59 us
    another operation x2 -> x0, other arithmetic: 1.59 us -> none  [coefficients(): parts = jnp.stack([diag, kappa * (1.0 / 16.0), rho * (1.0 / 216.0)], axis=1)]
    pad x2 -> x0, local copies, waits for them, and re-layouts: 1.48 us -> none  [the longest x1 0.74 us: per_device(): z_layer = jnp.pad(eigvecs[:, :, 0], ((0, 0), (0, edge - size_y), (0, 0)))]
  transfers between devices with their start and end apart: 3 -> 0, of which waited for: 2 -> 0; matrix products, arithmetic and copies ran while one was open for 4% -> 0% of each run, Pallas kernels for 0% -> 0%
where the time goes in v2:
time: 72.9 us; the launch traced here: 71.5 us
  Pallas kernels  68.3 us (94%)
  local copies, waits for them, and re-layouts  2.59 us (4%)
    pallas_call x1, Pallas kernels, per_device(): pl.pallas_call(functools.partial(kernel, 0.5 / total_cells, (nx, ny, nz))...  68.3 us
    unnamed x2, local copies, waits for them, and re-layouts  2.59 us

profile of v2, /device:TPU:1, one launch (start us, length us, event | category | flops | bytes accessed | tf_op | source)
XLA Modules:
  0.0 71.5 jit_solution(10528007339950650220)
XLA Ops:
  0.6 68.3 %shard_map.59 = (f32[4,512]{1,0:T(4,128)}, f32[4,512]{1,0:T(4,128)}) custom-call(bf16[16,384,512]{2,1,0:T(8,128)(2,1)} %bitcast.2, f32[2,128,48]{2,1,0:T(8,128)} %bitcast.3, bf16[2,2,384,512]{3,2,1,0:T(8,128)(2,1)} %constant.4.clone.t_hbm, f32[256,128]{1,0:T(8,128)} %constant.5.clone.w_ref), custom_call_target="tpu_custom_call" | custom-call | tf_op jit(solution)/shard_map/pallas_call | solution.py:502
  68.9 1.3 %copy.8 = f32[4,512]{1,0:T(4,128)} copy(f32[4,512]{1,0:T(4,128)} %get-tuple-element.4) | data formatting | bytes 16384
  70.2 1.3 %copy.9 = f32[4,512]{1,0:T(4,128)} copy(f32[4,512]{1,0:T(4,128)} %get-tuple-element.5) | data formatting | bytes 16384

commit v3 on v2

--- a/solution.py
+++ b/solution.py
@@ -144,8 +144,8 @@
             ref[...] = jnp.zeros(ref.shape, ref.dtype)
 
 
-def kernel(scale, sizes, v_ref, m_ref, t_hbm, w_ref, stiff_out, mass_out,
-           e, t, zl, zn, cz, cn, zx, cx, faces, kall, coef, u, ybuf, acc, blocks,
+def kernel(scale, sizes, v_ref, m_ref, t_hbm, w_ref, out,
+           e, t, ztile, zl, zn, cz, cn, zx, cx, faces, kall, coef, u, ybuf, acc, blocks,
            own_sem, v_send, v_recv, k_send, k_recv, *reduce_bufs):
     nx, ny, nz = sizes
     columns = e.shape[2]
@@ -157,7 +157,10 @@
     own = [pltpu.make_async_copy(v_ref.at[:, :hy], e.at[pl.ds(1, nx), low], own_sem.at[0]),
            pltpu.make_async_copy(v_ref.at[:, hy:], e.at[pl.ds(1, nx), high], own_sem.at[1]),
            pltpu.make_async_copy(t_hbm.at[gz], t, own_sem.at[2])]
-    for copy in own:
+    z_first = pl.multiple_of((nz - 16) * (1 - gz), 16)
+    tiles = [pltpu.make_async_copy(v_ref.at[:, pl.ds(y * nz + z_first, 16)], ztile.at[y], own_sem.at[3 + y])
+             for y in range(ny)]
+    for copy in tiles + own:
         copy.start()
     total = greet_around()
 
@@ -166,21 +169,21 @@
         faces[n] = jnp.concatenate([kappa[x * ny + y:x * ny + y + 1] for x in range(nx)], 0)
     kall[0, :cells] = kappa
 
-    row = lax.broadcasted_iota(jnp.int32, (nz, nz), 0)
-    col = lax.broadcasted_iota(jnp.int32, (nz, nz), 1)
-    exact = functools.partial(lax.dot_general, dimension_numbers=(((1,), (1,)), ((), ())),
-                              precision=lax.Precision.HIGHEST, preferred_element_type=jnp.float32)
-    unit = jnp.where(row == col, 1.0, 0.0)
-
-    def fill_coefficients(n, field):
-        for x in range(nx):
-            for y in range(ny):
-                at = x * ny + y
-                coef[n, x, y * nz:(y + 1) * nz] = jnp.broadcast_to(field[:, at:at + 1], (nz, 128))
-
-    flipped = exact(unit, kappa)
-    fill_coefficients(1, flipped * (1.0 / 16.0))
-    fill_coefficients(2, exact(unit, m_ref[1]) * (1.0 / 216.0))
+    for copy in tiles:
+        copy.wait()
+
+    def extract(at):
+        def edge_row(x, y):
+            return ztile[y, x].astype(jnp.float32)[at:at + 1]
+
+        for q in range(nx // 2):
+            rows = [edge_row(2 * q + n // ny, n % ny) for n in range(2 * ny)]
+            zl[q] = jnp.concatenate(rows, 0).astype(zl.dtype)
+        for n, y in enumerate((0, ny - 1)):
+            cz[n] = jnp.concatenate([edge_row(x, y) for x in range(nx)], 0).astype(cz.dtype)
+
+    pl.when(gz == 0)(functools.partial(extract, 15))
+    pl.when(gz == 1)(functools.partial(extract, 0))
 
     pl.semaphore_wait(pltpu.get_barrier_semaphore(), total)
 
@@ -229,10 +232,33 @@
         waits[0 if a < 0 else steps - 1].extend(made)
         begin(made)
 
+    def z_chunk(i):
+        first, last = (0, 2) if i == 0 else (i + 1, i + 2)
+        made = [vh.add((0, 0, 1), zl.at[pl.ds(first, last - first)], zn.at[pl.ds(first, last - first)])]
+        waits[i].extend(made)
+        begin(made)
+
+    def z_corners(a):
+        if a == 0:
+            made = [vh.add((0, b, 1), cz.at[y_face[b]], cn.at[which[b]]) for b in (-1, 1)]
+        else:
+            made = [vh.add((a, 0, 1), zl.at[nx // 2 - 1 if a < 0 else 0], zx.at[which[a]])]
+            made += [vh.add((a, b, 1), cz.at[y_face[b]], cx.at[which[a], which[b]]) for b in (-1, 1)]
+        waits[0 if a <= 0 else steps - 1].extend(made)
+        begin(made)
+
+    z_chunk(0)
+    z_corners(0)
+    z_corners(-1)
     y_chunk(0)
     x_plane(-1)
-    for i in range(1, steps):
+    for i in range(1, steps - 1):
+        z_chunk(i)
         y_chunk(i)
+        if i == steps // 2:
+            z_corners(1)
+            x_plane(1)
+    y_chunk(steps - 1)
     for b in (-1, 1):
         zero_unless(inside(0, b), [e.at[pl.ds(1, nx), y_dst[b]]])
     for a in (-1, 1):
@@ -243,46 +269,21 @@
         zero_unless(inside(0, b), [cn.at[which[b]]])
     acc[...] = jnp.zeros_like(acc)
 
-    own[0].wait()
-    own[1].wait()
-
-    def edge_row(x, y, z):
-        at = own_row(y, ny, nz) + z
-        first = at // 16 * 16
-        return e[x + 1, first:first + 16].astype(jnp.float32)[at - first:at - first + 1]
-
-    def extract(z):
-        for q in range(nx // 2):
-            rows = [edge_row(2 * q + n // ny, n % ny, z) for n in range(2 * ny)]
-            zl[q] = jnp.concatenate(rows, 0).astype(zl.dtype)
-        for n, y in enumerate((0, ny - 1)):
-            cz[n] = jnp.concatenate([edge_row(x, y, z) for x in range(nx)], 0).astype(cz.dtype)
-
-    pl.when(gz == 0)(functools.partial(extract, nz - 1))
-    pl.when(gz == 1)(functools.partial(extract, 0))
-
-    def z_chunk(i):
-        first, last = (0, 2) if i == 0 else (i + 1, i + 2)
-        made = [vh.add((0, 0, 1), zl.at[pl.ds(first, last - first)], zn.at[pl.ds(first, last - first)])]
-        waits[i].extend(made)
-        begin(made)
-
-    def z_corners(a):
-        if a == 0:
-            made = [vh.add((0, b, 1), cz.at[y_face[b]], cn.at[which[b]]) for b in (-1, 1)]
-        else:
-            made = [vh.add((a, 0, 1), zl.at[nx // 2 - 1 if a < 0 else 0], zx.at[which[a]])]
-            made += [vh.add((a, b, 1), cz.at[y_face[b]], cx.at[which[a], which[b]]) for b in (-1, 1)]
-        waits[0 if a <= 0 else steps - 1].extend(made)
-        begin(made)
-
-    z_chunk(0)
-    z_corners(0)
-    z_corners(-1)
-    for i in range(1, steps - 1):
-        z_chunk(i)
-    z_corners(1)
-    x_plane(1)
+    row = lax.broadcasted_iota(jnp.int32, (nz, nz), 0)
+    col = lax.broadcasted_iota(jnp.int32, (nz, nz), 1)
+    exact = functools.partial(lax.dot_general, dimension_numbers=(((1,), (1,)), ((), ())),
+                              precision=lax.Precision.HIGHEST, preferred_element_type=jnp.float32)
+    unit = jnp.where(row == col, 1.0, 0.0)
+
+    def fill_coefficients(n, field):
+        for x in range(nx):
+            for y in range(ny):
+                at = x * ny + y
+                coef[n, x, y * nz:(y + 1) * nz] = jnp.broadcast_to(field[:, at:at + 1], (nz, 128))
+
+    flipped = exact(unit, kappa)
+    fill_coefficients(1, flipped * (1.0 / 16.0))
+    fill_coefficients(2, exact(unit, m_ref[1]) * (1.0 / 216.0))
 
     arrive(kh.all)
     edge_from = jnp.where(gz == 0, nz - 1, 0)
@@ -292,7 +293,8 @@
     field = lax.dot_general(along_z, w_ref[...], (((1,), (0,)), ((), ())),
                             precision=lax.Precision.HIGHEST, preferred_element_type=jnp.float32)
     fill_coefficients(0, 2.0 * flipped + (1.0 / 32.0) * field)
-    own[2].wait()
+    for copy in own:
+        copy.wait()
 
     lane = lax.broadcasted_iota(jnp.int32, (8, columns), 0)
 
@@ -360,7 +362,7 @@
         upper_rows = lax.broadcasted_iota(jnp.int32, stiff.shape, 2) < 4
         blocks[g // 2, g % 2, :, :, 0] = jnp.where(upper_rows, stiff, pltpu.roll(mass, 4, 2))
         blocks[g // 2, g % 2, :, :, 1] = jnp.where(upper_rows, pltpu.roll(stiff, 4, 2), mass)
-    reduce_blocks(blocks, stiff_out, mass_out, reduce_bufs)
+    reduce_blocks(blocks, out, reduce_bufs)
     kh.finish()
     vh.finish()
 
@@ -420,7 +422,7 @@
     return held
 
 
-def reduce_blocks(r, stiff_out, mass_out, bufs):
+def reduce_blocks(r, out, bufs):
     zl, core, cx, cy, zh = coordinates()
     rc, ha, ra1, ha1, ra2, ha2, ra3, hb, rb1, hb1, rb2, hb2, rb3, send, recv = bufs
     half = r.shape[-1] // 2
@@ -446,12 +448,8 @@
     a3 = spread("z", lambda p: ha2.at[p % 2, p // 2], ra3, *sems(3))
     hb2[...] = gathered(b2, hb1[cx], rb2)
     b3 = spread("y", lambda p: hb2.at[p], rb3, *sems(3))
-    done = gathered(a3, ha2[zl, zh], ra3)
-    stiff_out[:, :half] = done[:4]
-    mass_out[:, :half] = done[4:]
-    done = gathered(b3, hb2[cy], rb3)
-    stiff_out[:, half:] = done[:4]
-    mass_out[:, half:] = done[4:]
+    out[:, :half] = gathered(a3, ha2[zl, zh], ra3)
+    out[:, half:] = gathered(b3, hb2[cy], rb3)
     for copy in first[0] + first[1] + a1 + b1 + a2 + b2 + a3 + b3:
         copy.wait_send()
 
@@ -484,6 +482,7 @@
     scratch = [
         pltpu.VMEM((nx + 2, 2 * block, columns), bf16),
         pltpu.VMEM((2, ny * nz, 2 * block), bf16),
+        pltpu.VMEM((ny, nx, 16, columns), bf16),
         pltpu.VMEM((nx // 2, 2 * ny, columns), bf16),
         pltpu.VMEM((nx // 2, 2 * ny, columns), bf16),
         pltpu.VMEM((2, nx, columns), bf16),
@@ -497,17 +496,18 @@
         pltpu.VMEM((STEP * ny * nz, 2 * columns), bf16),
         pltpu.VMEM((columns, 2 * columns), f32),
         pltpu.VMEM((2, 2, 4, 4, 2, 8, columns), f32),
-        dma((3,)), dma((48,)), dma((48,)), dma((17,)), dma((17,)),
+        dma((3 + ny,)), dma((48,)), dma((48,)), dma((17,)), dma((17,)),
     ] + reduce_scratch(columns)
-    return tuple(pl.pallas_call(
+    both = pl.pallas_call(
         functools.partial(kernel, 0.5 / total_cells, (nx, ny, nz)),
-        out_shape=[jax.ShapeDtypeStruct((4, columns), f32)] * 2,
+        out_shape=jax.ShapeDtypeStruct((8, columns), f32),
         in_specs=[anywhere, vmem, anywhere, vmem],
-        out_specs=[vmem, vmem],
+        out_specs=vmem,
         scratch_shapes=scratch,
         compiler_params=pltpu.CompilerParams(
             vmem_limit_bytes=60 * 1024 * 1024, collective_id=0, has_side_effects=True),
-    )(eigvecs.reshape(nx, ny * nz, columns), material.reshape(2, cells, nz), taps, around))
+    )(eigvecs.reshape(nx, ny * nz, columns), material.reshape(2, cells, nz), taps, around)
+    return both[:4], both[4:]
 
 
 def solution(mesh):

time: 72.9 us -> 57.5 us (0.79); the launches traced: 71.5 us -> 57.2 us
  Pallas kernels: 68.3 us -> 55.2 us
  local copies, waits for them, and re-layouts: 2.59 us -> 1.4 us
    pallas_call x1, Pallas kernels: 68.3 us -> 55.2 us  [per_device(): pl.pallas_call(functools.partial(kernel, 0.5 / total_cells, (nx, ny, nz))...]
    unnamed x2 -> x0, local copies, waits for them, and re-layouts: 2.59 us -> none
    slice x0 -> x1, local copies, waits for them, and re-layouts: none -> 1.4 us  [per_device(): return (both[:4], both[4:])]
where the time goes in v3:
time: 57.5 us; the launch traced here: 57.2 us
  Pallas kernels  55.2 us (96%)
  local copies, waits for them, and re-layouts  1.4 us (2%)
  between operations  0.64 us (1%)
    pallas_call x1, Pallas kernels, per_device(): pl.pallas_call(functools.partial(kernel, 0.5 / total_cells, (nx, ny, nz))...  55.2 us
    slice x1, local copies, waits for them, and re-layouts, per_device(): return (both[:4], both[4:])  1.4 us

profile of v3, /device:TPU:1, one launch (start us, length us, event | category | flops | bytes accessed | tf_op | source)
XLA Modules:
  0.0 57.2 jit_solution(13684187348556512746)
XLA Ops:
  0.6 55.2 %shard_map.59 = f32[8,512]{1,0:T(8,128)} custom-call(bf16[16,384,512]{2,1,0:T(8,128)(2,1)} %bitcast.2, f32[2,128,48]{2,1,0:T(8,128)} %bitcast.3, bf16[2,2,384,512]{3,2,1,0:T(8,128)(2,1)} %constant.4.clone.t_hbm, f32[256,128]{1,0:T(8,128)} %constant.5.clone.w_ref), custom_call_target="tpu_custom_call" | custom-call | tf_op jit(solution)/shard_map/pallas_call | solution.py:501
  55.8 1.4 %fusion = (f32[4,512]{1,0:T(4,128)}, f32[4,512]{1,0:T(4,128)}) fusion(f32[8,512]{1,0:T(8,128)} %shard_map.59), kind=kLoop, calls=%fused_computation | loop fusion | bytes 32768 | tf_op jit(solution)/shard_map/slice | solution.py:510

commit v4 on v3

--- a/solution.py
+++ b/solution.py
@@ -9,7 +9,8 @@
 
 AXES = ("gx", "gy", "gz")
 MESH = pl.DeviceIdType.MESH
-NEAR = [(a, b, c) for c in (0, 1) for a in (-1, 0, 1) for b in (-1, 0, 1) if (a, b, c) != (0, 0, 0)]
+SIDES = [(0, -1, 0), (0, 1, 0), (0, 0, 1), (0, -1, 1), (0, 1, 1)]
+NEAR = SIDES + [(-1, 0, 0), (1, 0, 0)]
 STEP = 2
 
 
@@ -49,21 +50,21 @@
 
 def material_taps(size_x, size_y):
     cells = size_x * size_y
-    places = [(x, y) for x in range(size_x) for y in range(size_y)]
-    places += [(x, y) for x in (-1, size_x) for y in range(size_y)]
-    places += [(x, y) for y in (-1, size_y) for x in range(size_x)]
-    for x in (-1, size_x):
-        for y in (-1, size_y):
-            places += [(x, y) if n == (7 if x < 0 else 0) else None for n in range(8)]
-    rows = -(-len(places) // 128) * 128
-    taps = np.zeros((rows, cells), np.float32)
-    for row, place in enumerate(places):
-        if place is None:
-            continue
-        for x in range(size_x):
-            for y in range(size_y):
-                taps[row, x * size_y + y] = weight(x - place[0], 2.0) * weight(y - place[1], 2.0)
-    return taps
+    own = [(x, y) for x in range(size_x) for y in range(size_y)]
+    faces = [(x, y) for y in (-1, size_y) for x in range(size_x)]
+    rows = -(-(cells + 2 * size_x) // 128) * 128
+    along_y = np.zeros((rows, cells), np.float32)
+    for row, (near_x, near_y) in enumerate(own + faces):
+        for col, (x, y) in enumerate(own):
+            if x == near_x:
+                along_y[row, col] = weight(y - near_y, 2.0)
+    along_x = np.zeros((3, cells, cells), np.float32)
+    for n, shift in enumerate((0, -size_x, size_x)):
+        for row, (near_x, near_y) in enumerate(own):
+            for col, (x, y) in enumerate(own):
+                if y == near_y:
+                    along_x[n, row, col] = weight(x - near_x - shift, 2.0)
+    return np.concatenate([along_y, along_x.reshape(3 * cells, cells)], 0)
 
 
 def inside(a, b):
@@ -145,7 +146,7 @@
 
 
 def kernel(scale, sizes, v_ref, m_ref, t_hbm, w_ref, out,
-           e, t, ztile, zl, zn, cz, cn, zx, cx, faces, kall, coef, u, ybuf, acc, blocks,
+           e, t, ztile, zl, zn, cz, cn, faces, kall, spans, coef, u, ybuf, acc, blocks,
            own_sem, v_send, v_recv, k_send, k_recv, *reduce_bufs):
     nx, ny, nz = sizes
     columns = e.shape[2]
@@ -188,83 +189,58 @@
     pl.semaphore_wait(pltpu.get_barrier_semaphore(), total)
 
     kh = Halo(k_send, k_recv)
-    x_tile = {-1: pl.ds(cells - ny, ny), 1: pl.ds(0, ny)}
-    f_tile = {-1: pl.ds(nx - 8, 8), 1: pl.ds(0, 8)}
     which = {-1: 0, 1: 1}
     y_face = {-1: 1, 1: 0}
-    for a, b, c in NEAR:
-        if (a, b) == (0, 0):
-            src, at, n = m_ref.at[0], 0, cells
-        elif b == 0:
-            src, at, n = m_ref.at[0, x_tile[a]], cells + which[a] * ny, ny
-        elif a == 0:
-            src, at, n = faces.at[y_face[b]], cells + 2 * ny + which[b] * nx, nx
+    for a, b, c in SIDES:
+        if b == 0:
+            src, dst = m_ref.at[0], kall.at[c, pl.ds(0, cells)]
         else:
-            src = faces.at[y_face[b], f_tile[a]]
-            at, n = cells + 2 * ny + 2 * nx + 8 * (2 * which[a] + which[b]), 8
-        dst = kall.at[c, pl.ds(at, n)]
+            src, dst = faces.at[y_face[b]], kall.at[c, pl.ds(cells + which[b] * nx, nx)]
         begin([kh.add((a, b, c), src, dst)])
         zero_unless(inside(a, b), [dst])
-    used = cells + 2 * ny + 2 * nx + 32
+    used = cells + 2 * nx
     for c in range(2):
         kall[c, used:] = jnp.zeros((kall.shape[1] - used, nz), jnp.float32)
 
     vh = Halo(v_send, v_recv)
     steps = nx // STEP
     waits = [[] for _ in range(steps)]
+    y_planes = [[(2 * i + 2, 2 * i + 4)] for i in range(steps - 1)] + [[]]
+    y_planes[0] = [(0, 4)]
+    y_planes[1].append((nx - 1, nx))
+    y_planes[steps - 2] = [(nx - 2, nx - 1)]
+    z_pairs = [[i + 1] for i in range(steps - 2)] + [[], []]
+    z_pairs[0] = [0, 1]
+    z_pairs[1].append(nx // 2 - 1)
     y_src = {-1: pl.ds((ny - 1) * nz, nz), 1: pl.ds(0, nz)}
     y_dst = {-1: pl.ds(0, nz), 1: pl.ds(block + hy, nz)}
-    x_src = {-1: nx - 1, 1: 0}
-    x_dst = {-1: 0, 1: nx + 1}
 
     def y_chunk(i):
-        first = 0 if i == 0 else STEP * i + 1
-        last = min(STEP * (i + 1) + 1, nx)
-        made = [vh.add((0, b, 0), v_ref.at[pl.ds(first, last - first), y_src[b]],
-                       e.at[pl.ds(first + 1, last - first), y_dst[b]]) for b in (-1, 1)]
-        waits[i].extend(made)
-        begin(made)
-
-    def x_plane(a):
-        made = [vh.add((a, 0, 0), v_ref.at[x_src[a], pl.ds(0, hy)], e.at[x_dst[a], low]),
-                vh.add((a, 0, 0), v_ref.at[x_src[a], pl.ds(hy, hy)], e.at[x_dst[a], high])]
-        made += [vh.add((a, b, 0), v_ref.at[x_src[a], y_src[b]], e.at[x_dst[a], y_dst[b]]) for b in (-1, 1)]
-        waits[0 if a < 0 else steps - 1].extend(made)
-        begin(made)
+        for first, last in y_planes[i]:
+            made = [vh.add((0, b, 0), v_ref.at[pl.ds(first, last - first), y_src[b]],
+                           e.at[pl.ds(first + 1, last - first), y_dst[b]]) for b in (-1, 1)]
+            waits[i].extend(made)
+            begin(made)
 
     def z_chunk(i):
-        first, last = (0, 2) if i == 0 else (i + 1, i + 2)
-        made = [vh.add((0, 0, 1), zl.at[pl.ds(first, last - first)], zn.at[pl.ds(first, last - first)])]
-        waits[i].extend(made)
-        begin(made)
-
-    def z_corners(a):
-        if a == 0:
-            made = [vh.add((0, b, 1), cz.at[y_face[b]], cn.at[which[b]]) for b in (-1, 1)]
-        else:
-            made = [vh.add((a, 0, 1), zl.at[nx // 2 - 1 if a < 0 else 0], zx.at[which[a]])]
-            made += [vh.add((a, b, 1), cz.at[y_face[b]], cx.at[which[a], which[b]]) for b in (-1, 1)]
-        waits[0 if a <= 0 else steps - 1].extend(made)
-        begin(made)
-
-    z_chunk(0)
-    z_corners(0)
-    z_corners(-1)
-    y_chunk(0)
-    x_plane(-1)
-    for i in range(1, steps - 1):
+        for pair in z_pairs[i]:
+            made = [vh.add((0, 0, 1), zl.at[pair], zn.at[pair])]
+            waits[i].extend(made)
+            begin(made)
+
+    corners = [vh.add((0, b, 1), cz.at[y_face[b]], cn.at[which[b]]) for b in (-1, 1)]
+    waits[0].extend(corners)
+    begin(corners)
+    for i in range(steps):
         z_chunk(i)
         y_chunk(i)
-        if i == steps // 2:
-            z_corners(1)
-            x_plane(1)
-    y_chunk(steps - 1)
+    x_below = vh.add((1, 0, 0), e.at[1], e.at[nx + 1])
+    x_above = vh.add((-1, 0, 0), e.at[nx], e.at[0])
+    waits[steps - 1].extend([x_below, x_above])
+    for a, at in ((-1, 0), (1, nx + 1)):
+        zero_unless(inside(a, 0), [e.at[at]])
     for b in (-1, 1):
         zero_unless(inside(0, b), [e.at[pl.ds(1, nx), y_dst[b]]])
-    for a in (-1, 1):
-        zero_unless(inside(a, 0), [e.at[x_dst[a], low], e.at[x_dst[a], high], zx.at[which[a]]])
-        for b in (-1, 1):
-            zero_unless(inside(a, b), [e.at[x_dst[a], y_dst[b]], cx.at[which[a], which[b]]])
     for b in (-1, 1):
         zero_unless(inside(0, b), [cn.at[which[b]]])
     acc[...] = jnp.zeros_like(acc)
@@ -275,39 +251,42 @@
                               precision=lax.Precision.HIGHEST, preferred_element_type=jnp.float32)
     unit = jnp.where(row == col, 1.0, 0.0)
 
-    def fill_coefficients(n, field):
-        for x in range(nx):
+    def fill_coefficients(n, field, planes):
+        for x in planes:
             for y in range(ny):
                 at = x * ny + y
                 coef[n, x, y * nz:(y + 1) * nz] = jnp.broadcast_to(field[:, at:at + 1], (nz, 128))
 
     flipped = exact(unit, kappa)
-    fill_coefficients(1, flipped * (1.0 / 16.0))
-    fill_coefficients(2, exact(unit, m_ref[1]) * (1.0 / 216.0))
+    fill_coefficients(1, flipped * (1.0 / 16.0), range(nx))
+    fill_coefficients(2, exact(unit, m_ref[1]) * (1.0 / 216.0), range(nx))
 
     arrive(kh.all)
     edge_from = jnp.where(gz == 0, nz - 1, 0)
     near_z = jnp.where(jnp.abs(row - col) == 1, 1.0, 0.0) + 2.0 * unit
     across = jnp.where(jnp.logical_and(row == edge_from, col == nz - 1 - edge_from), 1.0, 0.0)
     along_z = exact(near_z, kall[0]) + exact(across, kall[1])
-    field = lax.dot_general(along_z, w_ref[...], (((1,), (0,)), ((), ())),
-                            precision=lax.Precision.HIGHEST, preferred_element_type=jnp.float32)
-    fill_coefficients(0, 2.0 * flipped + (1.0 / 32.0) * field)
+    wide = kall.shape[1]
+    plain = functools.partial(jnp.dot, precision=lax.Precision.HIGHEST, preferred_element_type=jnp.float32)
+    spans[0] = plain(along_z, w_ref[:wide])
+
+    def diagonal(kappa, field):
+        return 2.0 * kappa + (1.0 / 32.0) * field
+
+    inner = plain(spans[0], w_ref[wide:wide + cells])
+    fill_coefficients(0, diagonal(flipped, inner), range(1, nx - 1))
+    spreads = [kh.add((a, 0, 0), spans.at[0], spans.at[1 + which[a]]) for a in (-1, 1)]
+    begin(spreads)
+    for a in (-1, 1):
+        zero_unless(inside(a, 0), [spans.at[1 + which[a]]])
     for copy in own:
         copy.wait()
 
     lane = lax.broadcasted_iota(jnp.int32, (8, columns), 0)
 
     def fill_edge(x):
-        if x < 0:
-            z8 = zx[0].astype(jnp.float32)[8:]
-            corners = [cx[0, n].astype(jnp.float32)[nx - 1:] for n in range(2)]
-        elif x == nx:
-            z8 = zx[1].astype(jnp.float32)[:8]
-            corners = [cx[1, n].astype(jnp.float32)[:1] for n in range(2)]
-        else:
-            z8 = zn[x // 2].astype(jnp.float32)[8 * (x % 2):8 * (x % 2) + 8]
-            corners = [cn[n].astype(jnp.float32)[x:x + 1] for n in range(2)]
+        z8 = zn[x // 2].astype(jnp.float32)[8 * (x % 2):8 * (x % 2) + 8]
+        corners = [cn[n].astype(jnp.float32)[x:x + 1] for n in range(2)]
         c8 = jnp.where(lane == 0, corners[0], jnp.where(lane == 1, corners[1], 0.0))
         full = jnp.concatenate([z8, c8], 0).astype(e.dtype)
         e[x + 1, block - 16:block] = full
@@ -328,13 +307,23 @@
             @pl.when(i == c)
             def _(c=c):
                 arrive(waits[c])
-                first = -1 if c == 0 else STEP * c + 1
-                for x in range(first, STEP * (c + 1) + 1):
-                    fill_edge(x)
+                for first, last in y_planes[c]:
+                    for x in range(first, last):
+                        fill_edge(x)
+                if c == 1:
+                    begin([x_below])
+                if c == 2:
+                    begin([x_above])
+                if c == steps - 1:
+                    arrive(spreads)
+                    field = plain(spans[0], w_ref[wide:wide + cells])
+                    for n in (1, 2):
+                        field = field + plain(spans[n], w_ref[wide + n * cells:wide + (n + 1) * cells])
+                    fill_coefficients(0, diagonal(exact(unit, m_ref[0]), field), (0, nx - 1))
 
         held = []
         for j in range(STEP):
-            x = STEP * i + j
+            x = lax.rem(STEP * i + j + 1, nx)
             here = e[x + 1]
             twice = here + here
             two = e[x] + e[x + 2] + twice
@@ -353,16 +342,23 @@
 
     lax.fori_loop(0, steps, iteration, 0)
 
-    for g in range(columns // 128):
-        some = slice(g * 128, (g + 1) * 128)
-        stiff = (acc[some, :columns] + acc[:, some].T) * scale
-        mass = (acc[some, columns:] + acc[:, columns + g * 128:columns + (g + 1) * 128].T) * scale
-        stiff = stiff.reshape(4, 4, 8, columns)
-        mass = mass.reshape(4, 4, 8, columns)
+    core = lax.axis_index("gx") % 2
+
+    def symmetric(zl_at, core_at):
+        some = pl.ds(pl.multiple_of((2 * zl_at + core_at) * 128, 128), 128)
+        also = pl.ds(pl.multiple_of((2 * zl_at + core_at) * 128 + columns, 128), 128)
+        stiff = ((acc[some, :columns] + acc[:, some].T) * scale).reshape(4, 4, 8, columns)
+        mass = ((acc[some, columns:] + acc[:, also].T) * scale).reshape(4, 4, 8, columns)
         upper_rows = lax.broadcasted_iota(jnp.int32, stiff.shape, 2) < 4
-        blocks[g // 2, g % 2, :, :, 0] = jnp.where(upper_rows, stiff, pltpu.roll(mass, 4, 2))
-        blocks[g // 2, g % 2, :, :, 1] = jnp.where(upper_rows, pltpu.roll(stiff, 4, 2), mass)
-    reduce_blocks(blocks, out, reduce_bufs)
+        blocks[zl_at, core_at, :, :, 0] = jnp.where(upper_rows, stiff, pltpu.roll(mass, 4, 2))
+        blocks[zl_at, core_at, :, :, 1] = jnp.where(upper_rows, pltpu.roll(stiff, 4, 2), mass)
+
+    for zl_at in range(2):
+        symmetric(zl_at, 1 - core)
+    first = send_across(blocks, reduce_bufs)
+    for zl_at in range(2):
+        symmetric(zl_at, core)
+    reduce_blocks(blocks, out, reduce_bufs, first)
     kh.finish()
     vh.finish()
 
@@ -372,29 +368,32 @@
     return gx // 2, gx % 2, gy // 4, gy % 4, gz
 
 
-def places_along(axis):
+def places_along(axes):
     zl, core, cx, cy, zh = coordinates()
-    count = 2 if axis == "core" else 4
-    me = {"core": core, "x": cx, "y": cy, "z": zh * 2 + zl}[axis]
+    if axes == "core":
+        peer = 1 - core
+        return [(peer, {"gx": zl * 2 + peer})]
+    me = {"x": cx, "y": cy, "z": zh * 2 + zl}
     found = []
-    for k in range(1, count):
-        peer = lax.rem(me + k, count)
-        if axis == "core":
-            device = {"gx": zl * 2 + peer}
-        elif axis == "x":
-            device = {"gy": peer * 4 + cy}
-        elif axis == "y":
-            device = {"gy": cx * 4 + peer}
-        else:
-            device = {"gx": (peer % 2) * 2 + core, "gz": peer // 2}
-        found.append((peer, device))
+    for k in range(1, 4 ** len(axes)):
+        at = dict(me)
+        for n, axis in enumerate(axes):
+            at[axis] = lax.rem(me[axis] + (k >> 2 * n) % 4, 4)
+        device = {}
+        if "x" in axes or "y" in axes:
+            device["gy"] = at["x"] * 4 + at["y"]
+        if "z" in axes:
+            device["gx"] = (at["z"] % 2) * 2 + core
+            device["gz"] = at["z"] // 2
+        peer = tuple(at[axis] for axis in axes)
+        found.append((peer if len(axes) > 1 else peer[0], device))
     return found
 
 
 def greet_reduction():
     barrier = pltpu.get_barrier_semaphore()
     total = 0
-    for axis in ("core", "x", "y", "z"):
+    for axis in ("core", "xy", "yz"):
         for _, device in places_along(axis):
             pl.semaphore_signal(barrier, inc=1, device_id=device, device_id_type=pl.DeviceIdType.MESH)
             total += 1
@@ -422,35 +421,31 @@
     return held
 
 
-def reduce_blocks(r, out, bufs):
+def lanes_of(columns):
+    return slice(0, columns // 2), slice(columns // 2, columns)
+
+
+def send_across(r, bufs):
+    rc, send, recv = bufs[0], bufs[-2], bufs[-1]
+    return [spread("core", lambda p, c=c: r.at[:, p, :, :, :, :, c], rc.at[i], send, recv, i)
+            for i, c in enumerate(lanes_of(r.shape[-1]))]
+
+
+def reduce_blocks(r, out, bufs, first):
     zl, core, cx, cy, zh = coordinates()
-    rc, ha, ra1, ha1, ra2, ha2, ra3, hb, rb1, hb1, rb2, hb2, rb3, send, recv = bufs
-    half = r.shape[-1] // 2
-    lanes = (slice(0, half), slice(half, 2 * half))
-    count = 0
-
-    def sems(n):
-        nonlocal count
-        count += n
-        return send, recv, count - n
-
-    first = [spread("core", lambda p, c=c: r.at[:, p, :, :, :, :, c], rc.at[i], *sems(1))
-             for i, c in enumerate(lanes)]
+    rc, ha, ra1, ha1, ra2, hb, rb1, hb1, rb2, send, recv = bufs
+    lanes = lanes_of(r.shape[-1])
     ha[...] = gathered(first[0], r[:, core, :, :, :, :, lanes[0]], rc.at[0])
-    a1 = spread("x", lambda p: ha.at[:, p], ra1, *sems(3))
+    a1 = spread("x", lambda p: ha.at[:, p], ra1, send, recv, 2)
     hb[...] = gathered(first[1], r[:, core, :, :, :, :, lanes[1]], rc.at[1])
-    b1 = spread("z", lambda p: hb.at[p % 2, :, :, p // 2], rb1, *sems(3))
+    b1 = spread("z", lambda p: hb.at[p % 2, :, :, p // 2], rb1, send, recv, 5)
     ha1[...] = gathered(a1, ha[:, cx], ra1)
-    a2 = spread("y", lambda p: ha1.at[:, p], ra2, *sems(3))
+    a2 = spread("yz", lambda p: ha1.at[p[1] % 2, p[0], p[1] // 2], ra2, send, recv, 8)
     hb1[...] = gathered(b1, hb[zl, :, :, zh], rb1)
-    b2 = spread("x", lambda p: hb1.at[p], rb2, *sems(3))
-    ha2[...] = gathered(a2, ha1[:, cy], ra2)
-    a3 = spread("z", lambda p: ha2.at[p % 2, p // 2], ra3, *sems(3))
-    hb2[...] = gathered(b2, hb1[cx], rb2)
-    b3 = spread("y", lambda p: hb2.at[p], rb3, *sems(3))
-    out[:, :half] = gathered(a3, ha2[zl, zh], ra3)
-    out[:, half:] = gathered(b3, hb2[cy], rb3)
-    for copy in first[0] + first[1] + a1 + b1 + a2 + b2 + a3 + b3:
+    b2 = spread("xy", lambda p: hb1.at[p[0], p[1]], rb2, send, recv, 23)
+    out[:, lanes[0]] = gathered(a2, ha1[zl, cy, zh], ra2)
+    out[:, lanes[1]] = gathered(b2, hb1[cx, cy], rb2)
+    for copy in first[0] + first[1] + a1 + b1 + a2 + b2:
         copy.wait_send()
 
 
@@ -458,11 +453,9 @@
     half = columns // 2
     f32 = jnp.float32
     shapes = [(2, 1, 2, 4, 4, 2, 8, half),
-              (2, 4, 4, 2, 8, half), (3, 2, 4, 2, 8, half), (2, 4, 2, 8, half), (3, 2, 2, 8, half),
-              (2, 2, 8, half), (3, 8, half),
-              (2, 4, 4, 2, 8, half), (3, 4, 4, 8, half), (4, 4, 8, half), (3, 4, 8, half),
-              (4, 8, half), (3, 8, half)]
-    return [pltpu.VMEM(shape, f32) for shape in shapes] + [pltpu.SemaphoreType.DMA((20,))] * 2
+              (2, 4, 4, 2, 8, half), (3, 2, 4, 2, 8, half), (2, 4, 2, 8, half), (15, 8, half),
+              (2, 4, 4, 2, 8, half), (3, 4, 4, 8, half), (4, 4, 8, half), (15, 8, half)]
+    return [pltpu.VMEM(shape, f32) for shape in shapes] + [pltpu.SemaphoreType.DMA((38,))] * 2
 
 
 def per_device(eigvecs, material):
@@ -487,16 +480,15 @@
         pltpu.VMEM((nx // 2, 2 * ny, columns), bf16),
         pltpu.VMEM((2, nx, columns), bf16),
         pltpu.VMEM((2, nx, columns), bf16),
-        pltpu.VMEM((2, 2 * ny, columns), bf16),
-        pltpu.VMEM((2, 2, nx, columns), bf16),
         pltpu.VMEM((2, nx, nz), f32),
-        pltpu.VMEM((2, around.shape[0], nz), f32),
+        pltpu.VMEM((2, around.shape[0] - 3 * cells, nz), f32),
+        pltpu.VMEM((3, nz, cells), f32),
         pltpu.VMEM((3, nx, ny * nz, 128), f32),
         pltpu.VMEM((STEP, 2, 2 * block, columns), bf16),
         pltpu.VMEM((STEP * ny * nz, 2 * columns), bf16),
         pltpu.VMEM((columns, 2 * columns), f32),
         pltpu.VMEM((2, 2, 4, 4, 2, 8, columns), f32),
-        dma((3 + ny,)), dma((48,)), dma((48,)), dma((17,)), dma((17,)),
+        dma((3 + ny,)), dma((32,)), dma((32,)), dma((7,)), dma((7,)),
     ] + reduce_scratch(columns)
     both = pl.pallas_call(
         functools.partial(kernel, 0.5 / total_cells, (nx, ny, nz)),

time: 57.5 us -> 56.2 us (0.977)
  Pallas kernels: 55.2 us -> 54 us
    pallas_call x1, Pallas kernels: 55.2 us -> 54 us  [per_device(): pl.pallas_call(functools.partial(kernel, 0.5 / total_cells, (nx, ny, nz))...]
where the time goes in v4:
time: 56.2 us; the launch traced here: 56 us
  Pallas kernels  54 us (96%)
  local copies, waits for them, and re-layouts  1.4 us (2%)
  between operations  0.64 us (1%)
    pallas_call x1, Pallas kernels, per_device(): pl.pallas_call(functools.partial(kernel, 0.5 / total_cells, (nx, ny, nz))...  54 us
    slice x1, local copies, waits for them, and re-layouts, per_device(): return (both[:4], both[4:])  1.4 us

profile of v4, /device:TPU:1, one launch (start us, length us, event | category | flops | bytes accessed | tf_op | source)
XLA Modules:
  0.0 56.0 jit_solution(15518081767050201558)
XLA Ops:
  0.6 54.0 %shard_map.59 = f32[8,512]{1,0:T(8,128)} custom-call(bf16[16,384,512]{2,1,0:T(8,128)(2,1)} %bitcast.2, f32[2,128,48]{2,1,0:T(8,128)} %bitcast.3, bf16[2,2,384,512]{3,2,1,0:T(8,128)(2,1)} %constant.4.clone.t_hbm, f32[640,128]{1,0:T(8,128)} %constant.5.clone.w_ref), custom_call_target="tpu_custom_call" | custom-call | tf_op jit(solution)/shard_map/pallas_call | solution.py:493
  54.6 1.4 %fusion = (f32[4,512]{1,0:T(4,128)}, f32[4,512]{1,0:T(4,128)}) fusion(f32[8,512]{1,0:T(8,128)} %shard_map.59), kind=kLoop, calls=%fused_computation | loop fusion | bytes 32768 | tf_op jit(solution)/shard_map/slice | solution.py:502

commit v5 on v4

--- a/solution.py
+++ b/solution.py
@@ -146,7 +146,7 @@
 
 
 def kernel(scale, sizes, v_ref, m_ref, t_hbm, w_ref, out,
-           e, t, ztile, zl, zn, cz, cn, faces, kall, spans, coef, u, ybuf, acc, blocks,
+           e, t, ztile, zl, zn, cz, cn, faces, kall, spans, coef, u, q, ybuf, acc,
            own_sem, v_send, v_recv, k_send, k_recv, *reduce_bufs):
     nx, ny, nz = sizes
     columns = e.shape[2]
@@ -251,34 +251,36 @@
                               precision=lax.Precision.HIGHEST, preferred_element_type=jnp.float32)
     unit = jnp.where(row == col, 1.0, 0.0)
 
-    def fill_coefficients(n, field, planes):
-        for x in planes:
-            for y in range(ny):
-                at = x * ny + y
-                coef[n, x, y * nz:(y + 1) * nz] = jnp.broadcast_to(field[:, at:at + 1], (nz, 128))
-
-    flipped = exact(unit, kappa)
-    fill_coefficients(1, flipped * (1.0 / 16.0), range(nx))
-    fill_coefficients(2, exact(unit, m_ref[1]) * (1.0 / 216.0), range(nx))
-
-    arrive(kh.all)
-    edge_from = jnp.where(gz == 0, nz - 1, 0)
-    near_z = jnp.where(jnp.abs(row - col) == 1, 1.0, 0.0) + 2.0 * unit
-    across = jnp.where(jnp.logical_and(row == edge_from, col == nz - 1 - edge_from), 1.0, 0.0)
-    along_z = exact(near_z, kall[0]) + exact(across, kall[1])
+    def keep(n, field):
+        for i in range(steps):
+            first = (STEP * i + 1) * ny
+            coef[n, i] = pltpu.roll(field, (cells - first) % cells, 1)
+
+    keep(1, exact(unit, kappa) * (1.0 / 16.0))
+    keep(2, exact(unit, m_ref[1]) * (1.0 / 216.0))
+
     wide = kall.shape[1]
     plain = functools.partial(jnp.dot, precision=lax.Precision.HIGHEST, preferred_element_type=jnp.float32)
-    spans[0] = plain(along_z, w_ref[:wide])
-
-    def diagonal(kappa, field):
-        return 2.0 * kappa + (1.0 / 32.0) * field
-
-    inner = plain(spans[0], w_ref[wide:wide + cells])
-    fill_coefficients(0, diagonal(flipped, inner), range(1, nx - 1))
+    near = list(kh.all)
     spreads = [kh.add((a, 0, 0), spans.at[0], spans.at[1 + which[a]]) for a in (-1, 1)]
-    begin(spreads)
     for a in (-1, 1):
         zero_unless(inside(a, 0), [spans.at[1 + which[a]]])
+
+    def tap_material():
+        arrive(near)
+        edge_from = jnp.where(gz == 0, nz - 1, 0)
+        near_z = jnp.where(jnp.abs(row - col) == 1, 1.0, 0.0) + 2.0 * unit
+        across = jnp.where(jnp.logical_and(row == edge_from, col == nz - 1 - edge_from), 1.0, 0.0)
+        along_z = exact(near_z, kall[0]) + exact(across, kall[1])
+        spans[0] = plain(along_z, w_ref[:wide])
+
+    def diagonal():
+        arrive(spreads)
+        field = plain(spans[0], w_ref[wide:wide + cells])
+        for n in (1, 2):
+            field = field + plain(spans[n], w_ref[wide + n * cells:wide + (n + 1) * cells])
+        keep(0, 2.0 * exact(unit, m_ref[0]) + (1.0 / 32.0) * field)
+
     for copy in own:
         copy.wait()
 
@@ -299,8 +301,17 @@
         three = jnp.dot(t[n, cut + 2 * nz:, block:], u[slot, n, block:], preferred_element_type=jnp.float32)
         return jnp.concatenate([one, two, three], 0)
 
-    def spread_lanes(c):
-        return jnp.concatenate([c] * (columns // 128), 1)
+    def coefficient(n, i, j):
+        field = coef[n, i]
+        tall = [jnp.broadcast_to(field[:, j * ny + y:j * ny + y + 1], (nz, 128)) for y in range(ny)]
+        return jnp.concatenate([jnp.concatenate(tall, 0)] * (columns // 128), 1)
+
+    def own_cells(x):
+        return jnp.concatenate([e[x + 1, nz:nz + hy], e[x + 1, block:block + hy]], 0)
+
+    def gram(n, cells_of):
+        acc[n] += lax.dot_general(jnp.concatenate(cells_of, 0), ybuf[n], (((0,), (0,)), ((), ())),
+                                  preferred_element_type=jnp.float32)
 
     def iteration(i, carry):
         for c in range(steps):
@@ -314,12 +325,10 @@
                     begin([x_below])
                 if c == 2:
                     begin([x_above])
-                if c == steps - 1:
-                    arrive(spreads)
-                    field = plain(spans[0], w_ref[wide:wide + cells])
-                    for n in (1, 2):
-                        field = field + plain(spans[n], w_ref[wide + n * cells:wide + (n + 1) * cells])
-                    fill_coefficients(0, diagonal(exact(unit, m_ref[0]), field), (0, nx - 1))
+                if c == 3:
+                    tap_material()
+                if c == 4:
+                    begin(spreads)
 
         held = []
         for j in range(STEP):
@@ -329,36 +338,59 @@
             two = e[x] + e[x + 2] + twice
             u[j, 0] = two
             u[j, 1] = two + twice
-            v = jnp.concatenate([here[nz:nz + hy], here[block:block + hy]], 0)
+            held.append(own_cells(x))
+            q[x] = (coefficient(1, i, j) * taps_of(0, j)).astype(q.dtype)
+            rows = slice(j * ny * nz, (j + 1) * ny * nz)
+            ybuf[0, rows] = (coefficient(2, i, j) * taps_of(1, j)).astype(ybuf.dtype)
+        gram(0, held)
+        return carry
+
+    def stiff_iteration(i, carry):
+        held = []
+        for j in range(STEP):
+            x = lax.rem(STEP * i + j + 1, nx)
+            v = own_cells(x)
             held.append(v)
-            rows = slice(j * ny * nz, (j + 1) * ny * nz)
-            stiff = spread_lanes(coef[0, x]) * v.astype(jnp.float32) - spread_lanes(coef[1, x]) * taps_of(0, j)
-            ybuf[rows, :columns] = stiff.astype(ybuf.dtype)
-            mass = spread_lanes(coef[2, x]) * taps_of(1, j)
-            ybuf[rows, columns:] = mass.astype(ybuf.dtype)
-        acc[...] += lax.dot_general(jnp.concatenate(held, 0), ybuf[...], (((0,), (0,)), ((), ())),
-                                    preferred_element_type=jnp.float32)
+            stiff = coefficient(0, i, j) * v.astype(jnp.float32) - q[x].astype(jnp.float32)
+            ybuf[1, j * ny * nz:(j + 1) * ny * nz] = stiff.astype(ybuf.dtype)
+        gram(1, held)
         return carry
 
     lax.fori_loop(0, steps, iteration, 0)
 
     core = lax.axis_index("gx") % 2
-
-    def symmetric(zl_at, core_at):
-        some = pl.ds(pl.multiple_of((2 * zl_at + core_at) * 128, 128), 128)
-        also = pl.ds(pl.multiple_of((2 * zl_at + core_at) * 128 + columns, 128), 128)
-        stiff = ((acc[some, :columns] + acc[:, some].T) * scale).reshape(4, 4, 8, columns)
-        mass = ((acc[some, columns:] + acc[:, also].T) * scale).reshape(4, 4, 8, columns)
-        upper_rows = lax.broadcasted_iota(jnp.int32, stiff.shape, 2) < 4
-        blocks[zl_at, core_at, :, :, 0] = jnp.where(upper_rows, stiff, pltpu.roll(mass, 4, 2))
-        blocks[zl_at, core_at, :, :, 1] = jnp.where(upper_rows, pltpu.roll(stiff, 4, 2), mass)
-
-    for zl_at in range(2):
-        symmetric(zl_at, 1 - core)
-    first = send_across(blocks, reduce_bufs)
-    for zl_at in range(2):
-        symmetric(zl_at, core)
-    reduce_blocks(blocks, out, reduce_bufs, first)
+    many = len(reduce_bufs) // 2
+    mass_bufs, stiff_bufs = reduce_bufs[:many], reduce_bufs[many:]
+
+    def symmetric(n, blocks, core_at):
+        for zl_at in range(2):
+            some = pl.ds(pl.multiple_of((2 * zl_at + core_at) * 128, 128), 128)
+            full = ((acc[n, some] + acc[n, :, some].T) * scale).reshape(4, 4, 8, columns)
+            left, right = full[..., :columns // 2], full[..., columns // 2:]
+            upper_rows = lax.broadcasted_iota(jnp.int32, left.shape, 2) < 4
+            blocks[zl_at, core_at, :, :, 0] = jnp.where(upper_rows, left, pltpu.roll(right, 4, 2))
+            blocks[zl_at, core_at, :, :, 1] = jnp.where(upper_rows, pltpu.roll(left, 4, 2), right)
+
+    symmetric(0, mass_bufs[0], 1 - core)
+    mass_sum = Reduction(mass_bufs)
+    mass_sum.across()
+    symmetric(0, mass_bufs[0], core)
+    diagonal()
+    some = steps * 5 // 8
+    lax.fori_loop(0, some, stiff_iteration, 0)
+    mass_sum.first()
+    lax.fori_loop(some, steps, stiff_iteration, 0)
+    symmetric(1, stiff_bufs[0], 1 - core)
+    stiff_sum = Reduction(stiff_bufs)
+    stiff_sum.across()
+    symmetric(1, stiff_bufs[0], core)
+    stiff_sum.first()
+    mass_sum.second()
+    stiff_sum.second()
+    mass_sum.store(out, 4)
+    stiff_sum.store(out, 0)
+    mass_sum.finish()
+    stiff_sum.finish()
     kh.finish()
     vh.finish()
 
@@ -421,38 +453,55 @@
     return held
 
 
-def lanes_of(columns):
-    return slice(0, columns // 2), slice(columns // 2, columns)
-
-
-def send_across(r, bufs):
-    rc, send, recv = bufs[0], bufs[-2], bufs[-1]
-    return [spread("core", lambda p, c=c: r.at[:, p, :, :, :, :, c], rc.at[i], send, recv, i)
-            for i, c in enumerate(lanes_of(r.shape[-1]))]
-
-
-def reduce_blocks(r, out, bufs, first):
-    zl, core, cx, cy, zh = coordinates()
-    rc, ha, ra1, ha1, ra2, hb, rb1, hb1, rb2, send, recv = bufs
-    lanes = lanes_of(r.shape[-1])
-    ha[...] = gathered(first[0], r[:, core, :, :, :, :, lanes[0]], rc.at[0])
-    a1 = spread("x", lambda p: ha.at[:, p], ra1, send, recv, 2)
-    hb[...] = gathered(first[1], r[:, core, :, :, :, :, lanes[1]], rc.at[1])
-    b1 = spread("z", lambda p: hb.at[p % 2, :, :, p // 2], rb1, send, recv, 5)
-    ha1[...] = gathered(a1, ha[:, cx], ra1)
-    a2 = spread("yz", lambda p: ha1.at[p[1] % 2, p[0], p[1] // 2], ra2, send, recv, 8)
-    hb1[...] = gathered(b1, hb[zl, :, :, zh], rb1)
-    b2 = spread("xy", lambda p: hb1.at[p[0], p[1]], rb2, send, recv, 23)
-    out[:, lanes[0]] = gathered(a2, ha1[zl, cy, zh], ra2)
-    out[:, lanes[1]] = gathered(b2, hb1[cx, cy], rb2)
-    for copy in first[0] + first[1] + a1 + b1 + a2 + b2:
-        copy.wait_send()
+class Reduction:
+    def __init__(self, bufs):
+        (self.r, self.rc, self.ha, self.ra1, self.ha1, self.ra2,
+         self.hb, self.rb1, self.hb1, self.rb2, self.send, self.recv) = bufs
+        half = self.r.shape[-1] // 2
+        self.lanes = slice(0, half), slice(half, 2 * half)
+        self.all = []
+
+    def spread(self, axes, piece, landing, base):
+        copies = spread(axes, piece, landing, self.send, self.recv, base)
+        self.all.extend(copies)
+        return copies
+
+    def across(self):
+        self.crossed = [self.spread("core", lambda p, c=c: self.r.at[:, p, :, :, :, :, c], self.rc.at[i], i)
+                        for i, c in enumerate(self.lanes)]
+
+    def first(self):
+        core = lax.axis_index("gx") % 2
+        self.ha[...] = gathered(self.crossed[0], self.r[:, core, :, :, :, :, self.lanes[0]], self.rc.at[0])
+        self.a1 = self.spread("x", lambda p: self.ha.at[:, p], self.ra1, 2)
+        self.hb[...] = gathered(self.crossed[1], self.r[:, core, :, :, :, :, self.lanes[1]], self.rc.at[1])
+        self.b1 = self.spread("z", lambda p: self.hb.at[p % 2, :, :, p // 2], self.rb1, 5)
+
+    def second(self):
+        zl, core, cx, cy, zh = coordinates()
+        self.ha1[...] = gathered(self.a1, self.ha[:, cx], self.ra1)
+        self.a2 = self.spread("yz", lambda p: self.ha1.at[p[1] % 2, p[0], p[1] // 2], self.ra2, 8)
+        self.hb1[...] = gathered(self.b1, self.hb[zl, :, :, zh], self.rb1)
+        self.b2 = self.spread("xy", lambda p: self.hb1.at[p[0], p[1]], self.rb2, 23)
+
+    def store(self, out, row):
+        zl, core, cx, cy, zh = coordinates()
+        half = out.shape[1] // 2
+        for lanes, copies, own, landing in ((self.lanes[0], self.a2, self.ha1[zl, cy, zh], self.ra2),
+                                            (self.lanes[1], self.b2, self.hb1[cx, cy], self.rb2)):
+            done = gathered(copies, own, landing)
+            out[row:row + 4, lanes] = done[:4]
+            out[row:row + 4, slice(half + lanes.start, half + lanes.stop)] = done[4:]
+
+    def finish(self):
+        for copy in self.all:
+            copy.wait_send()
 
 
 def reduce_scratch(columns):
-    half = columns // 2
+    half = columns // 4
     f32 = jnp.float32
-    shapes = [(2, 1, 2, 4, 4, 2, 8, half),
+    shapes = [(2, 2, 4, 4, 2, 8, 2 * half), (2, 1, 2, 4, 4, 2, 8, half),
               (2, 4, 4, 2, 8, half), (3, 2, 4, 2, 8, half), (2, 4, 2, 8, half), (15, 8, half),
               (2, 4, 4, 2, 8, half), (3, 4, 4, 8, half), (4, 4, 8, half), (15, 8, half)]
     return [pltpu.VMEM(shape, f32) for shape in shapes] + [pltpu.SemaphoreType.DMA((38,))] * 2
@@ -483,13 +532,13 @@
         pltpu.VMEM((2, nx, nz), f32),
         pltpu.VMEM((2, around.shape[0] - 3 * cells, nz), f32),
         pltpu.VMEM((3, nz, cells), f32),
-        pltpu.VMEM((3, nx, ny * nz, 128), f32),
+        pltpu.VMEM((3, nx // STEP, nz, cells), f32),
         pltpu.VMEM((STEP, 2, 2 * block, columns), bf16),
-        pltpu.VMEM((STEP * ny * nz, 2 * columns), bf16),
-        pltpu.VMEM((columns, 2 * columns), f32),
-        pltpu.VMEM((2, 2, 4, 4, 2, 8, columns), f32),
+        pltpu.VMEM((nx, ny * nz, columns), bf16),
+        pltpu.VMEM((2, STEP * ny * nz, columns), bf16),
+        pltpu.VMEM((2, columns, columns), f32),
         dma((3 + ny,)), dma((32,)), dma((32,)), dma((7,)), dma((7,)),
-    ] + reduce_scratch(columns)
+    ] + reduce_scratch(columns) * 2
     both = pl.pallas_call(
         functools.partial(kernel, 0.5 / total_cells, (nx, ny, nz)),
         out_shape=jax.ShapeDtypeStruct((8, columns), f32),

time: 56.2 us -> 57.1 us (1.016)
  Pallas kernels: 54 us -> 54.9 us
    pallas_call x1, Pallas kernels: 54 us -> 54.9 us  [per_device(): pl.pallas_call(functools.partial(kernel, 0.5 / total_cells, (nx, ny, nz))...]
where the time goes in v5:
time: 57.1 us; the launch traced here: 56.9 us
  Pallas kernels  54.9 us (96%)
  local copies, waits for them, and re-layouts  1.4 us (2%)
  between operations  0.64 us (1%)
    pallas_call x1, Pallas kernels, per_device(): pl.pallas_call(functools.partial(kernel, 0.5 / total_cells, (nx, ny, nz))...  54.9 us
    slice x1, local copies, waits for them, and re-layouts, per_device(): return (both[:4], both[4:])  1.4 us

profile of v5, /device:TPU:1, one launch (start us, length us, event | category | flops | bytes accessed | tf_op | source)
XLA Modules:
  0.0 56.9 jit_solution(956199857712479065)
XLA Ops:
  0.6 54.9 %shard_map.59 = f32[8,512]{1,0:T(8,128)} custom-call(bf16[16,384,512]{2,1,0:T(8,128)(2,1)} %bitcast.2, f32[2,128,48]{2,1,0:T(8,128)} %bitcast.3, bf16[2,2,384,512]{3,2,1,0:T(8,128)(2,1)} %constant.4.clone.t_hbm, f32[640,128]{1,0:T(8,128)} %constant.5.clone.w_ref), custom_call_target="tpu_custom_call" | custom-call | tf_op jit(solution)/shard_map/pallas_call | solution.py:542
  55.5 1.4 %fusion = (f32[4,512]{1,0:T(4,128)}, f32[4,512]{1,0:T(4,128)}) fusion(f32[8,512]{1,0:T(8,128)} %shard_map.59), kind=kLoop, calls=%fused_computation | loop fusion | bytes 32768 | tf_op jit(solution)/shard_map/slice | solution.py:551

commit v6 on v4

--- a/solution.py
+++ b/solution.py
@@ -96,6 +96,8 @@
     barrier = pltpu.get_barrier_semaphore()
     total = jnp.int32(greet_reduction())
     for a, b, c in NEAR:
+        if b and c:
+            continue
         there = inside(a, b)
 
         @when(there)
@@ -103,6 +105,21 @@
             pl.semaphore_signal(barrier, inc=1, device_id=device_at(a, b, c), device_id_type=MESH)
 
         total = total + (1 if there is None else jnp.where(there, 1, 0))
+    return total
+
+
+def vouch(far_sem):
+    total = jnp.int32(3)
+    for _, device in places_along("y"):
+        pl.semaphore_signal(far_sem, inc=1, device_id=device, device_id_type=MESH)
+    for b in (-1, 1):
+        there = inside(0, b)
+
+        @when(there)
+        def _(b=b):
+            pl.semaphore_signal(far_sem, inc=1, device_id=device_at(0, b, 0), device_id_type=MESH)
+
+        total = total + jnp.where(there, 1, 0)
     return total
 
 
@@ -147,7 +164,7 @@
 
 def kernel(scale, sizes, v_ref, m_ref, t_hbm, w_ref, out,
            e, t, ztile, zl, zn, cz, cn, faces, kall, spans, coef, u, ybuf, acc, blocks,
-           own_sem, v_send, v_recv, k_send, k_recv, *reduce_bufs):
+           own_sem, v_send, v_recv, k_send, k_recv, far_sem, *reduce_bufs):
     nx, ny, nz = sizes
     columns = e.shape[2]
     gz = lax.axis_index("gz")
@@ -187,17 +204,21 @@
     pl.when(gz == 1)(functools.partial(extract, 0))
 
     pl.semaphore_wait(pltpu.get_barrier_semaphore(), total)
+    vouched = vouch(far_sem)
 
     kh = Halo(k_send, k_recv)
     which = {-1: 0, 1: 1}
     y_face = {-1: 1, 1: 0}
-    for a, b, c in SIDES:
-        if b == 0:
-            src, dst = m_ref.at[0], kall.at[c, pl.ds(0, cells)]
-        else:
-            src, dst = faces.at[y_face[b]], kall.at[c, pl.ds(cells + which[b] * nx, nx)]
-        begin([kh.add((a, b, c), src, dst)])
-        zero_unless(inside(a, b), [dst])
+    def exchange_material(sides):
+        for a, b, c in sides:
+            if b == 0:
+                src, dst = m_ref.at[0], kall.at[c, pl.ds(0, cells)]
+            else:
+                src, dst = faces.at[y_face[b]], kall.at[c, pl.ds(cells + which[b] * nx, nx)]
+            begin([kh.add((a, b, c), src, dst)])
+            zero_unless(inside(a, b), [dst])
+
+    exchange_material([side for side in SIDES if not (side[1] and side[2])])
     used = cells + 2 * nx
     for c in range(2):
         kall[c, used:] = jnp.zeros((kall.shape[1] - used, nz), jnp.float32)
@@ -206,7 +227,7 @@
     steps = nx // STEP
     waits = [[] for _ in range(steps)]
     y_planes = [[(2 * i + 2, 2 * i + 4)] for i in range(steps - 1)] + [[]]
-    y_planes[0] = [(0, 4)]
+    y_planes[0] = [(0, 2), (2, 4)]
     y_planes[1].append((nx - 1, nx))
     y_planes[steps - 2] = [(nx - 2, nx - 1)]
     z_pairs = [[i + 1] for i in range(steps - 2)] + [[], []]
@@ -215,8 +236,8 @@
     y_src = {-1: pl.ds((ny - 1) * nz, nz), 1: pl.ds(0, nz)}
     y_dst = {-1: pl.ds(0, nz), 1: pl.ds(block + hy, nz)}
 
-    def y_chunk(i):
-        for first, last in y_planes[i]:
+    def y_chunk(i, planes=None):
+        for first, last in planes or y_planes[i]:
             made = [vh.add((0, b, 0), v_ref.at[pl.ds(first, last - first), y_src[b]],
                            e.at[pl.ds(first + 1, last - first), y_dst[b]]) for b in (-1, 1)]
             waits[i].extend(made)
@@ -228,15 +249,26 @@
             waits[i].extend(made)
             begin(made)
 
+    far = [(a, b, c) for a, b, c in SIDES if b and c]
+    z_chunk(0)
+    y_chunk(0, y_planes[0][:1])
+    pl.semaphore_wait(far_sem, vouched)
+    exchange_material(far)
     corners = [vh.add((0, b, 1), cz.at[y_face[b]], cn.at[which[b]]) for b in (-1, 1)]
     waits[0].extend(corners)
     begin(corners)
-    for i in range(steps):
+    y_chunk(0, y_planes[0][1:])
+    for i in range(1, steps):
         z_chunk(i)
         y_chunk(i)
-    x_below = vh.add((1, 0, 0), e.at[1], e.at[nx + 1])
-    x_above = vh.add((-1, 0, 0), e.at[nx], e.at[0])
-    waits[steps - 1].extend([x_below, x_above])
+    x_forward = {}
+    for a, mine, there in ((1, 0, nx + 1), (-1, nx - 1, 0)):
+        early = [vh.add((a, 0, 0), v_ref.at[mine, pl.ds(0, hy)], e.at[there, low]),
+                 vh.add((a, 0, 0), v_ref.at[mine, pl.ds(hy, hy)], e.at[there, high])]
+        begin(early)
+        x_forward[a] = [vh.add((a, 0, 0), e.at[mine + 1, rows], e.at[there, rows])
+                        for rows in (pl.ds(0, nz), pl.ds(nz + hy, 16), pl.ds(block + hy, nz + 16))]
+        waits[steps - 1].extend(early + x_forward[a])
     for a, at in ((-1, 0), (1, nx + 1)):
         zero_unless(inside(a, 0), [e.at[at]])
     for b in (-1, 1):
@@ -251,15 +283,14 @@
                               precision=lax.Precision.HIGHEST, preferred_element_type=jnp.float32)
     unit = jnp.where(row == col, 1.0, 0.0)
 
-    def fill_coefficients(n, field, planes):
-        for x in planes:
-            for y in range(ny):
-                at = x * ny + y
-                coef[n, x, y * nz:(y + 1) * nz] = jnp.broadcast_to(field[:, at:at + 1], (nz, 128))
+    def keep(n, field, only=None):
+        for i in range(steps) if only is None else only:
+            first = (STEP * i + 1) * ny
+            coef[n, i] = pltpu.roll(field, (cells - first) % cells, 1)
 
     flipped = exact(unit, kappa)
-    fill_coefficients(1, flipped * (1.0 / 16.0), range(nx))
-    fill_coefficients(2, exact(unit, m_ref[1]) * (1.0 / 216.0), range(nx))
+    keep(1, flipped * (1.0 / 16.0))
+    keep(2, exact(unit, m_ref[1]) * (1.0 / 216.0))
 
     arrive(kh.all)
     edge_from = jnp.where(gz == 0, nz - 1, 0)
@@ -274,9 +305,8 @@
         return 2.0 * kappa + (1.0 / 32.0) * field
 
     inner = plain(spans[0], w_ref[wide:wide + cells])
-    fill_coefficients(0, diagonal(flipped, inner), range(1, nx - 1))
+    keep(0, diagonal(flipped, inner))
     spreads = [kh.add((a, 0, 0), spans.at[0], spans.at[1 + which[a]]) for a in (-1, 1)]
-    begin(spreads)
     for a in (-1, 1):
         zero_unless(inside(a, 0), [spans.at[1 + which[a]]])
     for copy in own:
@@ -299,8 +329,10 @@
         three = jnp.dot(t[n, cut + 2 * nz:, block:], u[slot, n, block:], preferred_element_type=jnp.float32)
         return jnp.concatenate([one, two, three], 0)
 
-    def spread_lanes(c):
-        return jnp.concatenate([c] * (columns // 128), 1)
+    def coefficient(n, i, j):
+        field = coef[n, i]
+        tall = [jnp.broadcast_to(field[:, j * ny + y:j * ny + y + 1], (nz, 128)) for y in range(ny)]
+        return jnp.concatenate([jnp.concatenate(tall, 0)] * (columns // 128), 1)
 
     def iteration(i, carry):
         for c in range(steps):
@@ -311,15 +343,17 @@
                     for x in range(first, last):
                         fill_edge(x)
                 if c == 1:
-                    begin([x_below])
+                    begin(spreads)
                 if c == 2:
-                    begin([x_above])
-                if c == steps - 1:
+                    begin(x_forward[1])
+                if c == 3:
+                    begin(x_forward[-1])
+                if c == steps - 2:
                     arrive(spreads)
                     field = plain(spans[0], w_ref[wide:wide + cells])
                     for n in (1, 2):
                         field = field + plain(spans[n], w_ref[wide + n * cells:wide + (n + 1) * cells])
-                    fill_coefficients(0, diagonal(exact(unit, m_ref[0]), field), (0, nx - 1))
+                    keep(0, diagonal(exact(unit, m_ref[0]), field), (steps - 1,))
 
         held = []
         for j in range(STEP):
@@ -332,9 +366,9 @@
             v = jnp.concatenate([here[nz:nz + hy], here[block:block + hy]], 0)
             held.append(v)
             rows = slice(j * ny * nz, (j + 1) * ny * nz)
-            stiff = spread_lanes(coef[0, x]) * v.astype(jnp.float32) - spread_lanes(coef[1, x]) * taps_of(0, j)
+            stiff = coefficient(0, i, j) * v.astype(jnp.float32) - coefficient(1, i, j) * taps_of(0, j)
             ybuf[rows, :columns] = stiff.astype(ybuf.dtype)
-            mass = spread_lanes(coef[2, x]) * taps_of(1, j)
+            mass = coefficient(2, i, j) * taps_of(1, j)
             ybuf[rows, columns:] = mass.astype(ybuf.dtype)
         acc[...] += lax.dot_general(jnp.concatenate(held, 0), ybuf[...], (((0,), (0,)), ((), ())),
                                     preferred_element_type=jnp.float32)
@@ -393,7 +427,7 @@
 def greet_reduction():
     barrier = pltpu.get_barrier_semaphore()
     total = 0
-    for axis in ("core", "xy", "yz"):
+    for axis in ("core", "x", "y", "z"):
         for _, device in places_along(axis):
             pl.semaphore_signal(barrier, inc=1, device_id=device, device_id_type=pl.DeviceIdType.MESH)
             total += 1
@@ -483,12 +517,12 @@
         pltpu.VMEM((2, nx, nz), f32),
         pltpu.VMEM((2, around.shape[0] - 3 * cells, nz), f32),
         pltpu.VMEM((3, nz, cells), f32),
-        pltpu.VMEM((3, nx, ny * nz, 128), f32),
+        pltpu.VMEM((3, nx // STEP, nz, cells), f32),
         pltpu.VMEM((STEP, 2, 2 * block, columns), bf16),
         pltpu.VMEM((STEP * ny * nz, 2 * columns), bf16),
         pltpu.VMEM((columns, 2 * columns), f32),
         pltpu.VMEM((2, 2, 4, 4, 2, 8, columns), f32),
-        dma((3 + ny,)), dma((32,)), dma((32,)), dma((7,)), dma((7,)),
+        dma((3 + ny,)), dma((48,)), dma((48,)), dma((7,)), dma((7,)), pltpu.SemaphoreType.REGULAR,
     ] + reduce_scratch(columns)
     both = pl.pallas_call(
         functools.partial(kernel, 0.5 / total_cells, (nx, ny, nz)),

time: 56.2 us -> 54.6 us (0.972)
  Pallas kernels: 54 us -> 52.4 us
    pallas_call x1, Pallas kernels: 54 us -> 52.4 us  [per_device(): pl.pallas_call(functools.partial(kernel, 0.5 / total_cells, (nx, ny, nz))...]
where the time goes in v6:
time: 54.6 us; the launch traced here: 54.4 us
  Pallas kernels  52.4 us (96%)
  local copies, waits for them, and re-layouts  1.4 us (3%)
  between operations  0.64 us (1%)
    pallas_call x1, Pallas kernels, per_device(): pl.pallas_call(functools.partial(kernel, 0.5 / total_cells, (nx, ny, nz))...  52.4 us
    slice x1, local copies, waits for them, and re-layouts, per_device(): return (both[:4], both[4:])  1.4 us

profile of v6, /device:TPU:1, one launch (start us, length us, event | category | flops | bytes accessed | tf_op | source)
XLA Modules:
  0.0 54.4 jit_solution(18273352218590457772)
XLA Ops:
  0.6 52.4 %shard_map.59 = f32[8,512]{1,0:T(8,128)} custom-call(bf16[16,384,512]{2,1,0:T(8,128)(2,1)} %bitcast.2, f32[2,128,48]{2,1,0:T(8,128)} %bitcast.3, bf16[2,2,384,512]{3,2,1,0:T(8,128)(2,1)} %constant.4.clone.t_hbm, f32[640,128]{1,0:T(8,128)} %constant.5.clone.w_ref), custom_call_target="tpu_custom_call" | custom-call | tf_op jit(solution)/shard_map/pallas_call | solution.py:527
  53.0 1.4 %fusion = (f32[4,512]{1,0:T(4,128)}, f32[4,512]{1,0:T(4,128)}) fusion(f32[8,512]{1,0:T(8,128)} %shard_map.59), kind=kLoop, calls=%fused_computation | loop fusion | bytes 32768 | tf_op jit(solution)/shard_map/slice | solution.py:536

commit v7 on v6

--- a/solution.py
+++ b/solution.py
@@ -123,6 +123,11 @@
     return total
 
 
+def first_plane(i, steps):
+    late = i // (steps - 3) - i // (steps - 2)
+    return STEP * i + 1 - 2 * (i // (steps - 2)) + 4 * late
+
+
 class Halo:
     def __init__(self, send, recv):
         self.send, self.recv, self.count, self.all = send, recv, 0, []
@@ -163,7 +168,7 @@
 
 
 def kernel(scale, sizes, v_ref, m_ref, t_hbm, w_ref, out,
-           e, t, ztile, zl, zn, cz, cn, faces, kall, spans, coef, u, ybuf, acc, blocks,
+           e, t, ztile, zl, zn, cz, cn, faces, kall, spans, inner, coef, u, ybuf, acc, blocks,
            own_sem, v_send, v_recv, k_send, k_recv, far_sem, *reduce_bufs):
     nx, ny, nz = sizes
     columns = e.shape[2]
@@ -209,6 +214,8 @@
     kh = Halo(k_send, k_recv)
     which = {-1: 0, 1: 1}
     y_face = {-1: 1, 1: 0}
+    sent = []
+
     def exchange_material(sides):
         for a, b, c in sides:
             if b == 0:
@@ -216,6 +223,7 @@
             else:
                 src, dst = faces.at[y_face[b]], kall.at[c, pl.ds(cells + which[b] * nx, nx)]
             begin([kh.add((a, b, c), src, dst)])
+            sent.append((a, b, c))
             zero_unless(inside(a, b), [dst])
 
     exchange_material([side for side in SIDES if not (side[1] and side[2])])
@@ -226,11 +234,12 @@
     vh = Halo(v_send, v_recv)
     steps = nx // STEP
     waits = [[] for _ in range(steps)]
-    y_planes = [[(2 * i + 2, 2 * i + 4)] for i in range(steps - 1)] + [[]]
+    split = steps - 3
+    y_planes = [[(2 * i + 2, 2 * i + 4)] for i in range(split)] + [[], [(nx - 4, nx - 2)], []]
     y_planes[0] = [(0, 2), (2, 4)]
     y_planes[1].append((nx - 1, nx))
-    y_planes[steps - 2] = [(nx - 2, nx - 1)]
-    z_pairs = [[i + 1] for i in range(steps - 2)] + [[], []]
+    y_planes[2].append((nx - 2, nx - 1))
+    z_pairs = [[i + 1] for i in range(split)] + [[], [nx // 2 - 2], []]
     z_pairs[0] = [0, 1]
     z_pairs[1].append(nx // 2 - 1)
     y_src = {-1: pl.ds((ny - 1) * nz, nz), 1: pl.ds(0, nz)}
@@ -255,7 +264,6 @@
     pl.semaphore_wait(far_sem, vouched)
     exchange_material(far)
     corners = [vh.add((0, b, 1), cz.at[y_face[b]], cn.at[which[b]]) for b in (-1, 1)]
-    waits[0].extend(corners)
     begin(corners)
     y_chunk(0, y_planes[0][1:])
     for i in range(1, steps):
@@ -268,7 +276,7 @@
         begin(early)
         x_forward[a] = [vh.add((a, 0, 0), e.at[mine + 1, rows], e.at[there, rows])
                         for rows in (pl.ds(0, nz), pl.ds(nz + hy, 16), pl.ds(block + hy, nz + 16))]
-        waits[steps - 1].extend(early + x_forward[a])
+        waits[split].extend(early + x_forward[a])
     for a, at in ((-1, 0), (1, nx + 1)):
         zero_unless(inside(a, 0), [e.at[at]])
     for b in (-1, 1):
@@ -285,39 +293,74 @@
 
     def keep(n, field, only=None):
         for i in range(steps) if only is None else only:
-            first = (STEP * i + 1) * ny
+            first = first_plane(i, steps) * ny
             coef[n, i] = pltpu.roll(field, (cells - first) % cells, 1)
 
     flipped = exact(unit, kappa)
     keep(1, flipped * (1.0 / 16.0))
     keep(2, exact(unit, m_ref[1]) * (1.0 / 216.0))
 
-    arrive(kh.all)
+    material = {side: entry for side, entry in zip(sent, kh.all)}
+    arrive([material[side] for side in sent if side not in far])
     edge_from = jnp.where(gz == 0, nz - 1, 0)
     near_z = jnp.where(jnp.abs(row - col) == 1, 1.0, 0.0) + 2.0 * unit
     across = jnp.where(jnp.logical_and(row == edge_from, col == nz - 1 - edge_from), 1.0, 0.0)
-    along_z = exact(near_z, kall[0]) + exact(across, kall[1])
     wide = kall.shape[1]
     plain = functools.partial(jnp.dot, precision=lax.Precision.HIGHEST, preferred_element_type=jnp.float32)
-    spans[0] = plain(along_z, w_ref[:wide])
+    along_x = w_ref[wide:wide + cells]
+    along_z = exact(near_z, kall[0])
+    inner[0] = plain(along_z, w_ref[:wide]) + plain(exact(across, kall[1, :cells]), w_ref[:cells])
+    inner[1] = plain(inner[0], along_x)
 
     def diagonal(kappa, field):
         return 2.0 * kappa + (1.0 / 32.0) * field
 
-    inner = plain(spans[0], w_ref[wide:wide + cells])
-    keep(0, diagonal(flipped, inner))
+    keep(0, diagonal(flipped, inner[1]))
     spreads = [kh.add((a, 0, 0), spans.at[0], spans.at[1 + which[a]]) for a in (-1, 1)]
     for a in (-1, 1):
         zero_unless(inside(a, 0), [spans.at[1 + which[a]]])
+
+    def far_material():
+        arrive([material[side] for side in far])
+        here = plain(exact(across, kall[1, cells:]), w_ref[cells:wide])
+        spans[0] = inner[0] + here
+        keep(0, diagonal(exact(unit, m_ref[0]), inner[1] + plain(here, along_x)))
+
+    def along_planes(rows, middle):
+        return pltpu.roll(rows, 1, 0) + pltpu.roll(rows, nx - 1, 0) + middle * rows
+
+    def late_corners():
+        lanes = lax.broadcasted_iota(jnp.int32, (nx, nz), 1)
+        planes = lax.broadcasted_iota(jnp.int32, (nx, columns), 0)
+        done = jnp.logical_and(planes >= 1, planes <= 2 * STEP)
+
+        def at_edge(rows, edge):
+            return jnp.broadcast_to(jnp.sum(jnp.where(lanes == edge, rows, 0.0), axis=1, keepdims=True), (nx, columns))
+
+        added = []
+        for n, y in enumerate((0, ny - 1)):
+            rho = jnp.concatenate([m_ref[1, x * ny + y:x * ny + y + 1] for x in range(nx)], 0)
+            beyond = at_edge(kall[1, cells + n * nx:cells + (n + 1) * nx], nz - 1 - edge_from)
+            corner = cn[n].astype(jnp.float32)
+            stiff = (1.0 / 32.0) * along_planes(beyond, 2.0) * cz[n].astype(jnp.float32)
+            stiff = stiff - (1.0 / 16.0) * at_edge(faces[n], edge_from) * along_planes(corner, 2.0)
+            mass = (1.0 / 216.0) * at_edge(rho, edge_from) * along_planes(corner, 4.0)
+            added.append(jnp.concatenate([jnp.where(done, stiff, 0.0), jnp.where(done, mass, 0.0)], 1))
+        acc[...] += lax.dot_general(jnp.concatenate([cz[0], cz[1]], 0), jnp.concatenate(added, 0).astype(cz.dtype),
+                                    (((0,), (0,)), ((), ())), preferred_element_type=jnp.float32)
+
     for copy in own:
         copy.wait()
 
     lane = lax.broadcasted_iota(jnp.int32, (8, columns), 0)
 
-    def fill_edge(x):
+    def fill_edge(x, with_corners):
         z8 = zn[x // 2].astype(jnp.float32)[8 * (x % 2):8 * (x % 2) + 8]
-        corners = [cn[n].astype(jnp.float32)[x:x + 1] for n in range(2)]
-        c8 = jnp.where(lane == 0, corners[0], jnp.where(lane == 1, corners[1], 0.0))
+        if with_corners:
+            rows = [cn[n].astype(jnp.float32)[x:x + 1] for n in range(2)]
+            c8 = jnp.where(lane == 0, rows[0], jnp.where(lane == 1, rows[1], 0.0))
+        else:
+            c8 = jnp.zeros((8, columns), jnp.float32)
         full = jnp.concatenate([z8, c8], 0).astype(e.dtype)
         e[x + 1, block - 16:block] = full
         e[x + 1, 2 * block - 16:] = full
@@ -339,25 +382,27 @@
             @pl.when(i == c)
             def _(c=c):
                 arrive(waits[c])
-                for first, last in y_planes[c]:
-                    for x in range(first, last):
-                        fill_edge(x)
-                if c == 1:
-                    begin(spreads)
+                planes = [x for first, last in y_planes[c] for x in range(first, last)]
                 if c == 2:
-                    begin(x_forward[1])
+                    arrive(corners)
+                    planes += [x for k in range(2) for first, last in y_planes[k] for x in range(first, last)]
+                for x in planes:
+                    fill_edge(x, c >= 2)
+                if c == 2:
+                    far_material()
+                    late_corners()
                 if c == 3:
-                    begin(x_forward[-1])
-                if c == steps - 2:
+                    begin(spreads + x_forward[1] + x_forward[-1])
+                if c == split:
                     arrive(spreads)
-                    field = plain(spans[0], w_ref[wide:wide + cells])
+                    field = plain(spans[0], along_x)
                     for n in (1, 2):
                         field = field + plain(spans[n], w_ref[wide + n * cells:wide + (n + 1) * cells])
-                    keep(0, diagonal(exact(unit, m_ref[0]), field), (steps - 1,))
+                    keep(0, diagonal(exact(unit, m_ref[0]), field), (split,))
 
         held = []
         for j in range(STEP):
-            x = lax.rem(STEP * i + j + 1, nx)
+            x = lax.rem(first_plane(i, steps) + j, nx)
             here = e[x + 1]
             twice = here + here
             two = e[x] + e[x + 2] + twice
@@ -517,6 +562,7 @@
         pltpu.VMEM((2, nx, nz), f32),
         pltpu.VMEM((2, around.shape[0] - 3 * cells, nz), f32),
         pltpu.VMEM((3, nz, cells), f32),
+        pltpu.VMEM((2, nz, cells), f32),
         pltpu.VMEM((3, nx // STEP, nz, cells), f32),
         pltpu.VMEM((STEP, 2, 2 * block, columns), bf16),
         pltpu.VMEM((STEP * ny * nz, 2 * columns), bf16),

time: 54.6 us -> 56.7 us (1.038)
  Pallas kernels: 52.4 us -> 54.5 us
    pallas_call x1, Pallas kernels: 52.4 us -> 54.5 us  [per_device(): pl.pallas_call(functools.partial(kernel, 0.5 / total_cells, (nx, ny, nz))...]
where the time goes in v7:
time: 56.7 us; the launch traced here: 56.5 us
  Pallas kernels  54.5 us (96%)
  local copies, waits for them, and re-layouts  1.4 us (2%)
  between operations  0.64 us (1%)
    pallas_call x1, Pallas kernels, per_device(): pl.pallas_call(functools.partial(kernel, 0.5 / total_cells, (nx, ny, nz))...  54.5 us
    slice x1, local copies, waits for them, and re-layouts, per_device(): return (both[:4], both[4:])  1.4 us

profile of v7, /device:TPU:1, one launch (start us, length us, event | category | flops | bytes accessed | tf_op | source)
XLA Modules:
  0.0 56.5 jit_solution(14634505691557467124)
XLA Ops:
  0.6 54.5 %shard_map.59 = f32[8,512]{1,0:T(8,128)} custom-call(bf16[16,384,512]{2,1,0:T(8,128)(2,1)} %bitcast.2, f32[2,128,48]{2,1,0:T(8,128)} %bitcast.3, bf16[2,2,384,512]{3,2,1,0:T(8,128)(2,1)} %constant.4.clone.t_hbm, f32[640,128]{1,0:T(8,128)} %constant.5.clone.w_ref), custom_call_target="tpu_custom_call" | custom-call | tf_op jit(solution)/shard_map/pallas_call | solution.py:573
  55.1 1.4 %fusion = (f32[4,512]{1,0:T(4,128)}, f32[4,512]{1,0:T(4,128)}) fusion(f32[8,512]{1,0:T(8,128)} %shard_map.59), kind=kLoop, calls=%fused_computation | loop fusion | bytes 32768 | tf_op jit(solution)/shard_map/slice | solution.py:582

commit v8 on v6

--- a/solution.py
+++ b/solution.py
@@ -162,7 +162,7 @@
             ref[...] = jnp.zeros(ref.shape, ref.dtype)
 
 
-def kernel(scale, sizes, v_ref, m_ref, t_hbm, w_ref, out,
+def kernel(scale, sizes, v_ref, m_hbm, t_hbm, w_hbm, out, m_ref, w_ref,
            e, t, ztile, zl, zn, cz, cn, faces, kall, spans, coef, u, ybuf, acc, blocks,
            own_sem, v_send, v_recv, k_send, k_recv, far_sem, *reduce_bufs):
     nx, ny, nz = sizes
@@ -178,9 +178,12 @@
     z_first = pl.multiple_of((nz - 16) * (1 - gz), 16)
     tiles = [pltpu.make_async_copy(v_ref.at[:, pl.ds(y * nz + z_first, 16)], ztile.at[y], own_sem.at[3 + y])
              for y in range(ny)]
-    for copy in tiles + own:
+    own += [pltpu.make_async_copy(w_hbm, w_ref, own_sem.at[3 + ny])]
+    material_in = pltpu.make_async_copy(m_hbm, m_ref, own_sem.at[4 + ny])
+    for copy in [material_in] + tiles + own:
         copy.start()
     total = greet_around()
+    material_in.wait()
 
     kappa = m_ref[0]
     for n, y in enumerate((0, ny - 1)):
@@ -292,6 +295,7 @@
     keep(1, flipped * (1.0 / 16.0))
     keep(2, exact(unit, m_ref[1]) * (1.0 / 216.0))
 
+    own[3].wait()
     arrive(kh.all)
     edge_from = jnp.where(gz == 0, nz - 1, 0)
     near_z = jnp.where(jnp.abs(row - col) == 1, 1.0, 0.0) + 2.0 * unit
@@ -309,7 +313,7 @@
     spreads = [kh.add((a, 0, 0), spans.at[0], spans.at[1 + which[a]]) for a in (-1, 1)]
     for a in (-1, 1):
         zero_unless(inside(a, 0), [spans.at[1 + which[a]]])
-    for copy in own:
+    for copy in own[:3]:
         copy.wait()
 
     lane = lax.broadcasted_iota(jnp.int32, (8, columns), 0)
@@ -507,6 +511,8 @@
     vmem = pl.BlockSpec(memory_space=pltpu.VMEM)
     anywhere = pl.BlockSpec(memory_space=pl.ANY)
     scratch = [
+        pltpu.VMEM((2, cells, nz), f32),
+        pltpu.VMEM(around.shape, f32),
         pltpu.VMEM((nx + 2, 2 * block, columns), bf16),
         pltpu.VMEM((2, ny * nz, 2 * block), bf16),
         pltpu.VMEM((ny, nx, 16, columns), bf16),
@@ -522,12 +528,12 @@
         pltpu.VMEM((STEP * ny * nz, 2 * columns), bf16),
         pltpu.VMEM((columns, 2 * columns), f32),
         pltpu.VMEM((2, 2, 4, 4, 2, 8, columns), f32),
-        dma((3 + ny,)), dma((48,)), dma((48,)), dma((7,)), dma((7,)), pltpu.SemaphoreType.REGULAR,
+        dma((5 + ny,)), dma((48,)), dma((48,)), dma((7,)), dma((7,)), pltpu.SemaphoreType.REGULAR,
     ] + reduce_scratch(columns)
     both = pl.pallas_call(
         functools.partial(kernel, 0.5 / total_cells, (nx, ny, nz)),
-        out_shape=jax.ShapeDtypeStruct((8, columns), f32),
-        in_specs=[anywhere, vmem, anywhere, vmem],
+        out_shape=pltpu.VMEM((8, columns), f32),
+        in_specs=[anywhere] * 4,
         out_specs=vmem,
         scratch_shapes=scratch,
         compiler_params=pltpu.CompilerParams(

time: 54.6 us -> 52.2 us (0.956)
  Pallas kernels: 52.4 us -> 50.9 us
  local copies, waits for them, and re-layouts: 1.4 us -> 0.61 us
    pallas_call x1, Pallas kernels: 52.4 us -> 50.9 us  [per_device(): pl.pallas_call(functools.partial(kernel, 0.5 / total_cells, (nx, ny, nz))...]
    slice x1, local copies, waits for them, and re-layouts: 1.4 us -> 0.61 us  [per_device(): return (both[:4], both[4:])]
where the time goes in v8:
time: 52.2 us; the launch traced here: 52.1 us
  Pallas kernels  50.9 us (98%)
  between operations  0.64 us (1%)
  local copies, waits for them, and re-layouts  0.61 us (1%)
    pallas_call x1, Pallas kernels, per_device(): pl.pallas_call(functools.partial(kernel, 0.5 / total_cells, (nx, ny, nz))...  50.9 us

profile of v8, /device:TPU:1, one launch (start us, length us, event | category | flops | bytes accessed | tf_op | source)
XLA Modules:
  0.0 52.1 jit_solution(6932475072907284613)
XLA Ops:
  0.6 50.9 %shard_map.59 = f32[8,512]{1,0:T(8,128)S(1)} custom-call(bf16[16,384,512]{2,1,0:T(8,128)(2,1)} %bitcast.2, f32[2,128,48]{2,1,0:T(8,128)} %bitcast.3, bf16[2,2,384,512]{3,2,1,0:T(8,128)(2,1)} %constant.4.clone.t_hbm, f32[640,128]{1,0:T(8,128)} %constant.5.clone.w_hbm), custom_call_target="tpu_custom_call" | custom-call | tf_op jit(solution)/shard_map/pallas_call | solution.py:533
  51.5 0.6 %fusion = (f32[4,512]{1,0:T(4,128)}, f32[4,512]{1,0:T(4,128)}) fusion(f32[8,512]{1,0:T(8,128)S(1)} %shard_map.59), kind=kLoop, calls=%fused_computation | loop fusion | bytes 32768 | tf_op jit(solution)/shard_map/slice | solution.py:542

commit v9 on v8

--- a/solution.py
+++ b/solution.py
@@ -94,7 +94,7 @@
 
 def greet_around():
     barrier = pltpu.get_barrier_semaphore()
-    total = jnp.int32(greet_reduction())
+    total = jnp.int32(0)
     for a, b, c in NEAR:
         if b and c:
             continue
@@ -105,7 +105,7 @@
             pl.semaphore_signal(barrier, inc=1, device_id=device_at(a, b, c), device_id_type=MESH)
 
         total = total + (1 if there is None else jnp.where(there, 1, 0))
-    return total
+    return total + greet_reduction()
 
 
 def vouch(far_sem):
@@ -378,9 +378,10 @@
                                     preferred_element_type=jnp.float32)
         return carry
 
+    plan = plan_reduction(blocks, reduce_bufs)
     lax.fori_loop(0, steps, iteration, 0)
 
-    core = lax.axis_index("gx") % 2
+    core = plan[0][1]
 
     def symmetric(zl_at, core_at):
         some = pl.ds(pl.multiple_of((2 * zl_at + core_at) * 128, 128), 128)
@@ -393,12 +394,14 @@
 
     for zl_at in range(2):
         symmetric(zl_at, 1 - core)
-    first = send_across(blocks, reduce_bufs)
+    launch(plan[1][0] + plan[1][1])
     for zl_at in range(2):
         symmetric(zl_at, core)
-    reduce_blocks(blocks, out, reduce_bufs, first)
-    kh.finish()
-    vh.finish()
+    def finish():
+        kh.finish()
+        vh.finish()
+
+    reduce_blocks(blocks, out, reduce_bufs, plan, finish)
 
 
 def coordinates():
@@ -445,7 +448,6 @@
             src_ref=piece(peer), dst_ref=landing.at[k],
             send_sem=send.at[base + k], recv_sem=recv.at[base + k],
             device_id=device, device_id_type=pl.DeviceIdType.MESH)
-        copy.start()
         copies.append(copy)
     return copies
 
@@ -463,28 +465,46 @@
     return slice(0, columns // 2), slice(columns // 2, columns)
 
 
-def send_across(r, bufs):
-    rc, send, recv = bufs[0], bufs[-2], bufs[-1]
-    return [spread("core", lambda p, c=c: r.at[:, p, :, :, :, :, c], rc.at[i], send, recv, i)
-            for i, c in enumerate(lanes_of(r.shape[-1]))]
-
-
-def reduce_blocks(r, out, bufs, first):
-    zl, core, cx, cy, zh = coordinates()
+def launch(copies):
+    for copy in copies:
+        copy.start()
+
+
+def settle(copies):
+    for copy in copies:
+        copy.wait_send()
+
+
+def plan_reduction(r, bufs):
     rc, ha, ra1, ha1, ra2, hb, rb1, hb1, rb2, send, recv = bufs
+    first = [spread("core", lambda p, c=c: r.at[:, p, :, :, :, :, c], rc.at[i], send, recv, i)
+             for i, c in enumerate(lanes_of(r.shape[-1]))]
+    a1 = spread("x", lambda p: ha.at[:, p], ra1, send, recv, 2)
+    b1 = spread("z", lambda p: hb.at[p % 2, :, :, p // 2], rb1, send, recv, 5)
+    a2 = spread("yz", lambda p: ha1.at[p[1] % 2, p[0], p[1] // 2], ra2, send, recv, 8)
+    b2 = spread("xy", lambda p: hb1.at[p[0], p[1]], rb2, send, recv, 23)
+    return coordinates(), first, a1, b1, a2, b2
+
+
+def reduce_blocks(r, out, bufs, plan, finish):
+    rc, ha, ra1, ha1, ra2, hb, rb1, hb1, rb2, send, recv = bufs
+    (zl, core, cx, cy, zh), first, a1, b1, a2, b2 = plan
     lanes = lanes_of(r.shape[-1])
     ha[...] = gathered(first[0], r[:, core, :, :, :, :, lanes[0]], rc.at[0])
-    a1 = spread("x", lambda p: ha.at[:, p], ra1, send, recv, 2)
+    launch(a1)
     hb[...] = gathered(first[1], r[:, core, :, :, :, :, lanes[1]], rc.at[1])
-    b1 = spread("z", lambda p: hb.at[p % 2, :, :, p // 2], rb1, send, recv, 5)
+    launch(b1)
+    finish()
+    settle(first[0] + first[1])
     ha1[...] = gathered(a1, ha[:, cx], ra1)
-    a2 = spread("yz", lambda p: ha1.at[p[1] % 2, p[0], p[1] // 2], ra2, send, recv, 8)
+    launch(a2)
     hb1[...] = gathered(b1, hb[zl, :, :, zh], rb1)
-    b2 = spread("xy", lambda p: hb1.at[p[0], p[1]], rb2, send, recv, 23)
+    launch(b2)
+    settle(a1 + b1)
     out[:, lanes[0]] = gathered(a2, ha1[zl, cy, zh], ra2)
+    settle(a2)
     out[:, lanes[1]] = gathered(b2, hb1[cx, cy], rb2)
-    for copy in first[0] + first[1] + a1 + b1 + a2 + b2:
-        copy.wait_send()
+    settle(b2)
 
 
 def reduce_scratch(columns):

time: 52.2 us -> 52.2 us (level)
  no operation moved by 1% of the time
where the time goes in v9:
time: 52.2 us; the launch traced here: 52.1 us
  Pallas kernels  50.8 us (97%)
  between operations  0.64 us (1%)
  local copies, waits for them, and re-layouts  0.61 us (1%)
    pallas_call x1, Pallas kernels, per_device(): pl.pallas_call(functools.partial(kernel, 0.5 / total_cells, (nx, ny, nz))...  50.8 us

profile of v9, /device:TPU:1, one launch (start us, length us, event | category | flops | bytes accessed | tf_op | source)
XLA Modules:
  0.0 52.1 jit_solution(14842038807531364185)
XLA Ops:
  0.6 50.8 %shard_map.59 = f32[8,512]{1,0:T(8,128)S(1)} custom-call(bf16[16,384,512]{2,1,0:T(8,128)(2,1)} %bitcast.2, f32[2,128,48]{2,1,0:T(8,128)} %bitcast.3, bf16[2,2,384,512]{3,2,1,0:T(8,128)(2,1)} %constant.4.clone.t_hbm, f32[640,128]{1,0:T(8,128)} %constant.5.clone.w_hbm), custom_call_target="tpu_custom_call" | custom-call | tf_op jit(solution)/shard_map/pallas_call | solution.py:553
  51.5 0.6 %fusion = (f32[4,512]{1,0:T(4,128)}, f32[4,512]{1,0:T(4,128)}) fusion(f32[8,512]{1,0:T(8,128)S(1)} %shard_map.59), kind=kLoop, calls=%fused_computation | loop fusion | bytes 32768 | tf_op jit(solution)/shard_map/slice | solution.py:562

commit v10 on v9

--- a/solution.py
+++ b/solution.py
@@ -392,9 +392,10 @@
         blocks[zl_at, core_at, :, :, 0] = jnp.where(upper_rows, stiff, pltpu.roll(mass, 4, 2))
         blocks[zl_at, core_at, :, :, 1] = jnp.where(upper_rows, pltpu.roll(stiff, 4, 2), mass)
 
-    for zl_at in range(2):
-        symmetric(zl_at, 1 - core)
-    launch(plan[1][0] + plan[1][1])
+    symmetric(0, 1 - core)
+    launch(plan[1][0][:1])
+    symmetric(1, 1 - core)
+    launch(plan[1][0][1:] + plan[1][1])
     for zl_at in range(2):
         symmetric(zl_at, core)
     def finish():
@@ -475,10 +476,16 @@
         copy.wait_send()
 
 
+def crossed(copies, own, landing):
+    for copy in copies:
+        copy.wait_recv()
+    return own + landing[0]
+
+
 def plan_reduction(r, bufs):
     rc, ha, ra1, ha1, ra2, hb, rb1, hb1, rb2, send, recv = bufs
-    first = [spread("core", lambda p, c=c: r.at[:, p, :, :, :, :, c], rc.at[i], send, recv, i)
-             for i, c in enumerate(lanes_of(r.shape[-1]))]
+    first = [[spread("core", lambda p, c=c, z=z: r.at[z, p, :, :, :, :, c], rc.at[i, :, z], send, recv,
+                     i if z == 0 else 38 + i)[0] for z in range(2)] for i, c in enumerate(lanes_of(r.shape[-1]))]
     a1 = spread("x", lambda p: ha.at[:, p], ra1, send, recv, 2)
     b1 = spread("z", lambda p: hb.at[p % 2, :, :, p // 2], rb1, send, recv, 5)
     a2 = spread("yz", lambda p: ha1.at[p[1] % 2, p[0], p[1] // 2], ra2, send, recv, 8)
@@ -490,9 +497,9 @@
     rc, ha, ra1, ha1, ra2, hb, rb1, hb1, rb2, send, recv = bufs
     (zl, core, cx, cy, zh), first, a1, b1, a2, b2 = plan
     lanes = lanes_of(r.shape[-1])
-    ha[...] = gathered(first[0], r[:, core, :, :, :, :, lanes[0]], rc.at[0])
+    ha[...] = crossed(first[0], r[:, core, :, :, :, :, lanes[0]], rc.at[0])
     launch(a1)
-    hb[...] = gathered(first[1], r[:, core, :, :, :, :, lanes[1]], rc.at[1])
+    hb[...] = crossed(first[1], r[:, core, :, :, :, :, lanes[1]], rc.at[1])
     launch(b1)
     finish()
     settle(first[0] + first[1])
@@ -513,7 +520,7 @@
     shapes = [(2, 1, 2, 4, 4, 2, 8, half),
               (2, 4, 4, 2, 8, half), (3, 2, 4, 2, 8, half), (2, 4, 2, 8, half), (15, 8, half),
               (2, 4, 4, 2, 8, half), (3, 4, 4, 8, half), (4, 4, 8, half), (15, 8, half)]
-    return [pltpu.VMEM(shape, f32) for shape in shapes] + [pltpu.SemaphoreType.DMA((38,))] * 2
+    return [pltpu.VMEM(shape, f32) for shape in shapes] + [pltpu.SemaphoreType.DMA((40,))] * 2
 
 
 def per_device(eigvecs, material):

time: 52.2 us -> 52.1 us (level)
  no operation moved by 1% of the time
where the time goes in v10:
time: 52.1 us; the launch traced here: 52 us
  Pallas kernels  50.7 us (97%)
  between operations  0.64 us (1%)
  local copies, waits for them, and re-layouts  0.61 us (1%)
    pallas_call x1, Pallas kernels, per_device(): pl.pallas_call(functools.partial(kernel, 0.5 / total_cells, (nx, ny, nz))...  50.7 us

profile of v10, /device:TPU:1, one launch (start us, length us, event | category | flops | bytes accessed | tf_op | source)
XLA Modules:
  0.0 52.0 jit_solution(199249203575217472)
XLA Ops:
  0.6 50.7 %shard_map.59 = f32[8,512]{1,0:T(8,128)S(1)} custom-call(bf16[16,384,512]{2,1,0:T(8,128)(2,1)} %bitcast.2, f32[2,128,48]{2,1,0:T(8,128)} %bitcast.3, bf16[2,2,384,512]{3,2,1,0:T(8,128)(2,1)} %constant.4.clone.t_hbm, f32[640,128]{1,0:T(8,128)} %constant.5.clone.w_hbm), custom_call_target="tpu_custom_call" | custom-call | tf_op jit(solution)/shard_map/pallas_call | solution.py:560
  51.3 0.6 %fusion = (f32[4,512]{1,0:T(4,128)}, f32[4,512]{1,0:T(4,128)}) fusion(f32[8,512]{1,0:T(8,128)S(1)} %shard_map.59), kind=kLoop, calls=%fused_computation | loop fusion | bytes 32768 | tf_op jit(solution)/shard_map/slice | solution.py:569
